TPU v7x, 8 devices: a whole 2x2x1 slice. The times are simulated.
8 devices in a mesh: dp: 1 (over z), sp: 8 (over y, x, core).
Axes of the slice: x: 2, y: 2, z: 1, core: 2. Of those that a mesh axis runs over, the one named last changes fastest.
Arguments:
- tokens: bfloat16 [256, 2048], P('dp')
- w_query: bfloat16 [2048, 2048], replicated
- w_key: bfloat16 [2048, 256], replicated
- w_value: bfloat16 [2048, 256], replicated
- w_out: bfloat16 [2048, 2048], P('sp')
- k_cache: bfloat16 [256, 2048, 256], P('dp', 'sp')
- v_cache: bfloat16 [256, 2048, 256], P('dp', 'sp')
- positions: int32 [256], P('dp')
Outputs:
- output 1: bfloat16 [256, 2048], P('dp')
- output 2: bfloat16 [256, 2048, 256], P('dp', 'sp')
- output 3: bfloat16 [256, 2048, 256], P('dp', 'sp')
All inputs are finite; a program needn't handle non-finite values.
Results may differ from a plain program's by a relative error of at most 0.00427737.
Values are sent between devices in bfloat16 or wider.
A program may use at most 1 GiB of HBM per device.

v0:
```python
import jax
import jax.numpy as jnp
from jax import lax
from jax.sharding import PartitionSpec as P


def solution(mesh):
    def local_step(tokens, w_query, w_key, w_value, w_out, k_cache, v_cache, positions):
        n_rows, seq_local, head_dim = k_cache.shape
        q_width = w_query.shape[1]
        n_heads = q_width // head_dim
        rows_local = w_out.shape[0]
        shard_idx = lax.axis_index('sp')
        queries = jnp.dot(tokens, w_query, preferred_element_type=jnp.float32).astype(jnp.bfloat16).reshape(n_rows, n_heads, head_dim)
        key_new = jnp.dot(tokens, w_key, preferred_element_type=jnp.float32).astype(jnp.bfloat16)
        value_new = jnp.dot(tokens, w_value, preferred_element_type=jnp.float32).astype(jnp.bfloat16)
        local_pos = positions - shard_idx * seq_local
        slot_ids = jnp.arange(seq_local)
        hit_mask = (slot_ids[None, :] == local_pos[:, None])[:, :, None]
        k_upd = jnp.where(hit_mask, key_new[:, None, :], k_cache)
        v_upd = jnp.where(hit_mask, value_new[:, None, :], v_cache)
        scores = jnp.einsum('bhd,btd->bht', queries, k_upd, preferred_element_type=jnp.float32) * head_dim ** -0.5
        valid_mask = (slot_ids[None, :] <= local_pos[:, None])[:, None, :]
        scores = jnp.where(valid_mask, scores, -jnp.inf)
        row_peak = jnp.maximum(jnp.max(scores, axis=2), -1e30)
        weights = jnp.exp(scores - row_peak[:, :, None])
        weight_sum = jnp.sum(weights, axis=2)
        value_sum = jnp.einsum('bht,btd->bhd', weights.astype(jnp.bfloat16), v_upd, preferred_element_type=jnp.float32)
        peak_all = lax.pmax(row_peak, 'sp')
        rescale = jnp.exp(row_peak - peak_all)
        weight_all = lax.psum(weight_sum * rescale, 'sp')
        value_all = lax.psum(value_sum * rescale[:, :, None], 'sp')
        attn_heads = (value_all / weight_all[:, :, None]).astype(jnp.bfloat16).reshape(n_rows, q_width)
        attn_local = lax.dynamic_slice_in_dim(attn_heads, shard_idx * rows_local, rows_local, axis=1)
        partial = jnp.dot(attn_local, w_out, preferred_element_type=jnp.float32)
        attn_out = lax.psum(partial, 'sp').astype(jnp.bfloat16)
        return attn_out, k_upd, v_upd

    cache_spec = P('dp', 'sp', None)
    return jax.shard_map(local_step, mesh=mesh, in_specs=(P('dp', None), P(), P(), P(), P('sp', None), cache_spec, cache_spec, P('dp')), out_specs=(P('dp', None), cache_spec, cache_spec), check_vma=False)
```

profile of v0, /device:TPU:0, one launch (start us, length us, event | category | flops | bytes accessed | tf_op | source)
XLA Modules:
  0.0 218.6 jit_solution(8265458613102469539)
XLA Ops:
  7.2 0.0 copy-start
  7.2 0.0 copy-start.2
  7.2 0.0 all-reduce.3.cloned.1.call-start
  7.2 0.8 broadcast_subtract_fusion
  8.1 0.1 iota_compare_fusion.1
  8.2 0.2 copy-done
  8.4 1.7 convolution_convert_fusion.2
  10.1 0.0 copy-done.2
  10.1 0.4 convolution_convert_fusion.1
  10.5 5.7 %convolution_convert_fusion = bf16[256,2048]{1,0:T(8,128)(2,1)S(1)} fusion(bf16[256,2048]{1,0:T(8,128)(2,1)S(1)} %copy-done, bf16[2048,2048]{1,0:T(8,128)(2,1)} %param.9), kind=kOutput, calls=%fused_computation.2 | convolution fusion | flops 2148007936 | bytes 10485760 | tf_op jit(solution)/shard_map/dot_general | solution.py:14
  16.3 0.3 copy.11
  16.6 43.4 %broadcast_select_fusion.1 = (bf16[256,256,256]{2,1,0:T(8,128)(2,1)}, bf16[256,256,256]{2,1,0:T(8,128)(2,1)}) fusion(bf16[256,256,256]{2,1,0:T(8,128)(2,1)} %param.13, pred[256,256]{1,0:T(8,128)(4,1)S(1)} %get-tuple-element.8, bf16[256,256]{1,0:T(8,128)(2,1)S(1)} %convolution_convert_fusion.2, bf16[256,256,256]{2,1,0:T(8,128)(2,1)} %param.14, ...), kind=kLoop, calls=%fused_computation.1 | loop fusion | flops 33554432 | bytes 134545408 | tf_op jit(solution)/shard_map/jit(_where)/select_n | solution.py:20
  60.0 14.6 %fusion = (f32[256,8]{1,0:T(8,128)S(1)}, f32[256,8,256]{2,1,0:T(8,128)S(1)}) fusion(pred[256,256]{1,0:T(8,128)(4,1)S(1)} %get-tuple-element.7, bf16[256,8,256]{2,1,0:T(8,128)(2,1)S(1)} %bitcast.14, bf16[256,256,256]{2,1,0:T(8,128)(2,1)} %get-tuple-element.5), kind=kOutput, calls=%fused_computation.6 | convolution fusion | flops 270006272 | bytes 36773888 | tf_op jit(solution)/shard_map/bhd,btd->bht/dot_general | solution.py:22
  74.6 26.1 %pmax.7 = f32[256,8]{1,0:T(8,128)S(1)} all-reduce(f32[256,8]{1,0:T(8,128)S(1)} %broadcast_maximum_fusion), channel_id=1, replica_groups=mesh['dp'=1,'sp'=8] {'sp'}, use_global_device_ids=true, to_apply=%region_1.2 | all-reduce | flops 2048 | bytes 16384 | tf_op jit(solution)/shard_map/pmax | solution.py:29
  100.7 1.0 fusion.1
  101.7 14.4 %convolution_multiply_fusion = f32[256,8,256]{2,1,0:T(8,128)} fusion(bf16[256,256,256]{2,1,0:T(8,128)(2,1)} %get-tuple-element.6, f32[256,8,256]{2,1,0:T(8,128)S(1)} %get-tuple-element.10, f32[256,8]{1,0:T(8,128)S(1)} %get-tuple-element.4, f32[256,8]{1,0:T(8,128)S(1)} %broadcast_maximum_fusion, pred[256,256]{1,0:T(8,128)(4,1)S(1)} %get-tuple-element.7), kind=kOutput, calls=%fused_computation.9 | convolution fusion | flops 271056896 | bytes 37830656 | tf_op jit(solution)/shard_map/bht,btd->bhd/dot_general | solution.py:28
  116.1 0.0 all-reduce.3.cloned.1.call-update
  116.1 24.3 %psum.22 = f32[256,8]{1,0:T(8,128)S(1)} all-reduce(f32[256,8]{1,0:T(8,128)S(1)} %get-tuple-element.3), channel_id=1, replica_groups=mesh['dp'=1,'sp'=8] {'sp'}, use_global_device_ids=true, to_apply=%region_4.5 | all-reduce | flops 2048 | bytes 16384 | tf_op jit(solution)/shard_map/psum | solution.py:31
  140.4 27.5 %all-reduce.3.cloned.1.call-done = f32[256,8,256]{2,1,0:T(8,128)} async-done(((f32[256,8,256]{2,1,0:T(8,128)}), f32[256,8,256]{2,1,0:T(8,128)}) %all-reduce.3.cloned.1.call-update) | async-done | bytes 2097168 | tf_op jit(solution)/shard_map/psum | solution.py:32
  167.9 0.0 copy-start.3
  167.9 2.0 divide_convert_fusion
  169.9 0.3 copy.12
  170.2 0.0 copy-done.3
  170.2 0.0 copy-start.1
  170.2 0.4 fusion.8
  170.7 41.1 %all-reduce.4 = bf16[256,2048]{1,0:T(8,128)(2,1)} all-reduce(f32[256,2048]{1,0:T(8,128)S(1)} %fusion.8), channel_id=1, replica_groups=mesh['dp'=1,'sp'=8] {'sp'}, use_global_device_ids=true, to_apply=%region_5.6 | all-reduce | flops 524288 | bytes 3145728 | tf_op jit(solution)/shard_map/psum | solution.py:36
  211.8 0.0 copy-done.1
  (2 shorter events, 0.1 us)
Async XLA Ops:
  7.2 1.3 copy-start
  7.2 2.9 %copy-start.2 = (bf16[2048,256]{1,0:T(8,128)(2,1)S(1)}, bf16[2048,256]{1,0:T(8,128)(2,1)}, u32[]{:S(2)}) copy-start(bf16[2048,256]{1,0:T(8,128)(2,1)} %param.11) | copy-start | bytes 3145732
  7.2 160.7 %all-reduce.3.cloned.1.call-start = ((), (), s32[]{:S(2)}) async-start(), calls=%async_computation | async-start | bytes 4194304 | tf_op jit(solution)/shard_map/psum | solution.py:32
  167.9 2.3 %copy-start.3 = (bf16[256,2048]{1,0:T(8,128)(2,1)S(1)}, bf16[256,2048]{1,0:T(8,128)(2,1)}, u32[]{:S(2)}) copy-start(bf16[256,2048]{1,0:T(8,128)(2,1)} %param.12) | copy-start | bytes 3145732
  170.2 41.6 %copy-start.1 = (bf16[256,2048]{1,0:T(8,128)(2,1)S(1)}, bf16[256,2048]{1,0:T(8,128)(2,1)}, u32[]{:S(2)}) copy-start(bf16[256,2048]{1,0:T(8,128)(2,1)} %param.8) | copy-start | bytes 3145732
Sparse Core Ops, SparseCore 0:
  116.2 51.5 all-reduce.2
where the time goes:
time: 219 us
  blocking collectives  91.5 us (42%)
  other arithmetic  47.4 us (22%)
  matrix products  37.2 us (17%)
  waiting for transfers between devices  27.5 us (13%)
  between operations  14.2 us (6%)
    select_n x1, other arithmetic, local_step(): k_upd = jnp.where(hit_mask, key_new[:, None, :], k_cache)  43.4 us
    psum x1, blocking collectives, local_step(): attn_out = lax.psum(partial, 'sp').astype(jnp.bfloat16)  41.1 us
    psum x1, waiting for transfers between devices, local_step(): value_all = lax.psum(value_sum * rescale[:, :, None], 'sp')  27.5 us
    pmax x1, blocking collectives, local_step(): peak_all = lax.pmax(row_peak, 'sp')  26.1 us
    psum x1, blocking collectives, local_step(): weight_all = lax.psum(weight_sum * rescale, 'sp')  24.3 us
    dot_general x1, matrix products, local_step(): jnp.einsum('bhd,btd->bht', queries, k_upd, preferred_element_type=jnp.flo...  14.6 us
    dot_general x1, matrix products, local_step(): jnp.einsum('bht,btd->bhd', weights.astype(jnp.bfloat16), v_upd, preferred...  14.4 us
    dot_general x1, matrix products, local_step(): jnp.dot(tokens, w_query, preferred_element_type=jnp.float32)  5.71 us
  transfers between devices with their start and end apart: 1, of which 1 were waited for; matrix products, arithmetic and copies ran while one was open for 0% of the time, Pallas kernels for 0%

commit v1 on v0

v1 whole, which is shorter than its diff:
```python
import functools

import jax
import jax.numpy as jnp
from jax import lax
from jax.experimental import pallas as pl
from jax.experimental.pallas import tpu as pltpu
from jax.sharding import PartitionSpec as P

MESH = pl.DeviceIdType.MESH
F32, BF16 = jnp.float32, jnp.bfloat16
FLOOR = -1e30
HALF = 16
LAG_C, LAG_S, LAG_R = 3, 5, 7


def attend_kernel(dims, pos_ref, q_ref, kn_ref, vn_ref, wo_ref, k_hbm, v_hbm, y_ref, held,
                  part, got_d, mix, got_1, yp, got_2, ybuf, wo2, sem_k, sem_v, sem_w,
                  snd_d, rcv_d, snd_1, rcv_1, snd_2, rcv_2, snd_3, rcv_3, snd_r, rcv_r):
    n_seq, heads, seq_local, hd, groups, slots = dims
    nh, width = HALF, wo_ref.shape[1]
    kb, vb = held.at[0], held.at[1]
    n_blocks, quarter = 2 * groups, width // 4
    body = heads * nh
    scale = hd ** -0.5
    me = lax.axis_index('sp')
    chip, core = me // 2, lax.rem(me, 2)

    def peer(k):
        return {'sp': jnp.bitwise_xor(me, k)}

    def cache_copies(t):
        s = lax.rem(t, slots)
        rows = pl.ds(t * nh, nh)
        return (pltpu.make_async_copy(k_hbm.at[rows], kb.at[s], sem_k.at[s]),
                pltpu.make_async_copy(v_hbm.at[rows], vb.at[s], sem_v.at[s]))

    def load(t):
        for cp in cache_copies(t):
            cp.start()

    for t in range(min(slots, n_blocks)):
        load(t)

    gate = pltpu.get_barrier_semaphore()
    for k in (1, 2, 4, 6):
        pl.semaphore_signal(gate, inc=1, device_id=peer(k), device_id_type=MESH)
    pl.semaphore_wait(gate, 4)

    send_w = pltpu.make_async_remote_copy(wo_ref, wo2.at[core], sem_w.at[0], sem_w.at[1],
                                          device_id=peer(1), device_id_type=MESH)
    send_w.start()
    keep_w = pltpu.make_async_copy(wo_ref, wo2.at[core], sem_w.at[2])

    def d_copy(g):
        return pltpu.make_async_remote_copy(part.at[g, 1 - core], got_d.at[g], snd_d.at[g], rcv_d.at[g],
                                            device_id=peer(1), device_id_type=MESH)

    def one_copy(g, k):
        return pltpu.make_async_remote_copy(mix.at[g, jnp.bitwise_xor(chip, k)], got_1.at[g, k - 1],
                                            snd_1.at[g, k - 1], rcv_1.at[g, k - 1],
                                            device_id=peer(2 * k), device_id_type=MESH)

    def two_copy(g, k):
        return pltpu.make_async_remote_copy(yp.at[g, jnp.bitwise_xor(chip, k)], got_2.at[g, k - 1],
                                            snd_2.at[g, k - 1], rcv_2.at[g, k - 1],
                                            device_id=peer(2 * k), device_id_type=MESH)

    def three_copy(g, k):
        block = ybuf.at[2 * g + core, :, pl.ds(pl.multiple_of(chip * quarter, quarter), quarter)]
        return pltpu.make_async_remote_copy(block, block, snd_3.at[g, k - 1], rcv_3.at[g, k - 1],
                                            device_id=peer(2 * k), device_id_type=MESH)

    def relay_copy(g):
        rows = ybuf.at[2 * g + core]
        return pltpu.make_async_remote_copy(rows, rows, snd_r.at[g], rcv_r.at[g],
                                            device_id=peer(1), device_id_type=MESH)

    slot_ids = lax.broadcasted_iota(jnp.int32, (heads, seq_local), 1)
    lane = lax.broadcasted_iota(jnp.int32, (heads, 128), 1)

    def attend(g, half):
        t = 2 * g + half
        s = lax.rem(t, slots)
        for cp in cache_copies(t):
            cp.wait()
        first = pl.multiple_of(t * nh, nh)
        kn, vn = kn_ref[pl.ds(first, nh), :], vn_ref[pl.ds(first, nh), :]
        scores = []
        for i in range(nh):
            scores.append(lax.dot_general(q_ref[first + i], kb[s, i], (((1,), (1,)), ((), ())),
                                          preferred_element_type=F32) * scale)
        peaks = jnp.full((heads, 128), FLOOR, F32)
        sums = jnp.zeros((heads, 128), F32)
        weights = []
        for i in range(nh):
            p = pos_ref[first + i]
            own = jnp.logical_and(p >= 0, p < seq_local)
            sc = jnp.where(slot_ids < p, scores[i], -jnp.inf)
            fresh = jnp.sum(q_ref[first + i].astype(F32) * kn[i:i + 1, :], axis=1, keepdims=True) * scale
            fresh = jnp.where(own, fresh, -jnp.inf)
            m = jnp.maximum(jnp.maximum(jnp.max(sc, axis=1, keepdims=True), fresh), FLOOR)
            w, wf = jnp.exp(sc - m), jnp.exp(fresh - m)
            peaks = jnp.where(lane == i, m, peaks)
            sums = jnp.where(lane == i, jnp.sum(w, axis=1, keepdims=True) + wf, sums)
            weights.append((w.astype(BF16), wf.astype(BF16).astype(F32)))
        for i in range(nh):
            w, wf = weights[i]
            o = jnp.dot(w, vb[s, i], preferred_element_type=F32) + wf * vn[i:i + 1, :]
            for z in range(2):
                part[g, half, z, pl.ds(i, heads, stride=nh), :] = o[:, z * 128:(z + 1) * 128]
        part[g, half, 0, body:body + heads, :] = peaks
        part[g, half, 1, body:body + heads, :] = sums

        @pl.when(t + slots < n_blocks)
        def _():
            load(t + slots)

    def merge(g):
        d_copy(g).wait_recv()
        a, b = part.at[g, core], got_d.at[g]
        tail = slice(body, body + heads)
        m = jnp.maximum(a[0, tail, :], b[0, tail, :])
        ea, eb = jnp.exp(a[0, tail, :] - m), jnp.exp(b[0, tail, :] - m)
        total = a[1, tail, :] * ea + b[1, tail, :] * eb
        cols = jnp.transpose(jnp.concatenate([ea, eb], axis=0))
        for h in range(heads):
            rows = slice(h * nh, (h + 1) * nh)
            ca = jnp.broadcast_to(cols[:nh, h:h + 1], (nh, 128))
            cb = jnp.broadcast_to(cols[:nh, heads + h:heads + h + 1], (nh, 128))
            for z in range(2):
                mix[g, h // 2, z, (h % 2) * nh:(h % 2 + 1) * nh, :] = a[z, rows, :] * ca + b[z, rows, :] * cb
        for z, ml in enumerate((m, total)):
            for c in range(4):
                rolled = ml if c == 0 else jnp.concatenate([ml[2 * c:], ml[:2 * c]], axis=0)
                mix[g, c, z, 2 * nh:2 * nh + heads, :] = rolled

    def project(g):
        for k in (1, 2, 3):
            one_copy(g, k).wait_recv()
        parts = [mix.at[g, chip]] + [got_1.at[g, k] for k in range(3)]
        tail = slice(2 * nh, 2 * nh + heads)
        peaks = [r[0, tail, :] for r in parts]
        m = functools.reduce(jnp.maximum, peaks)
        es = [jnp.exp(x - m) for x in peaks]
        total = sum(e * r[1, tail, :] for e, r in zip(es, parts))
        total = jnp.where(total > 0, total, 1.0)
        cols = jnp.transpose(jnp.concatenate([e / total for e in es], axis=0))
        outs = []
        for j in range(2):
            cs = [jnp.broadcast_to(cols[:nh, i * heads + j:i * heads + j + 1], (nh, 128)) for i in range(4)]
            o = [sum(r[z, j * nh:(j + 1) * nh, :] * c for r, c in zip(parts, cs)) for z in range(2)]
            outs.append(jnp.concatenate(o, axis=1).astype(BF16))
        for c in range(4):
            w = slice(c * quarter, (c + 1) * quarter)
            yp[g, c] = (jnp.dot(outs[0], wo2[0, :, w], preferred_element_type=F32)
                        + jnp.dot(outs[1], wo2[1, :, w], preferred_element_type=F32))

    def settle(g):
        for k in (1, 2, 3):
            two_copy(g, k).wait_recv()
        y = yp[g, chip] + got_2[g, 0] + got_2[g, 1] + got_2[g, 2]
        ybuf[2 * g + core, :, pl.ds(pl.multiple_of(chip * quarter, quarter), quarter)] = y.astype(BF16)

    keep_w.start()

    def step(it, carry):
        @pl.when(it < groups)
        def _():
            lax.fori_loop(0, 2, lambda half, c: (attend(it, half), c)[1], 0)
            d_copy(it).start()

        @pl.when(jnp.logical_and(it >= 1, it < groups + 1))
        def _():
            merge(it - 1)

        @pl.when(it == LAG_C)
        def _():
            keep_w.wait()
            send_w.wait()

        @pl.when(jnp.logical_and(it >= 1, it < groups + 1))
        def _():
            for k in (3, 1, 2):
                one_copy(it - 1, k).start()

        @pl.when(jnp.logical_and(it >= LAG_C, it < groups + LAG_C))
        def _():
            project(it - LAG_C)
            for k in (3, 1, 2):
                two_copy(it - LAG_C, k).start()

        @pl.when(jnp.logical_and(it >= LAG_S, it < groups + LAG_S))
        def _():
            settle(it - LAG_S)
            for k in (3, 1, 2):
                three_copy(it - LAG_S, k).start()

        @pl.when(it >= LAG_R)
        def _():
            for k in (1, 2, 3):
                three_copy(it - LAG_R, k).wait_recv()
            relay_copy(it - LAG_R).start()
        return carry

    lax.fori_loop(0, groups + LAG_R, step, 0)

    def finish(g, carry):
        relay_copy(g).wait()
        d_copy(g).wait_send()
        for k in (1, 2, 3):
            one_copy(g, k).wait_send()
            two_copy(g, k).wait_send()
            three_copy(g, k).wait_send()
        return carry

    lax.fori_loop(0, groups, finish, 0)
    y_ref[...] = ybuf[...]


def write_kernel(dims, pos_ref, kn_ref, vn_ref, held, k_hbm, v_hbm, ko_hbm, vo_hbm,
                 kc, vc, k_slab, v_slab, sem_in, sem_out, sem_keep, sem_slab):
    n_seq, seq_local, n_blocks, slots = dims
    nh = HALF
    step = nh // 2
    kr, vr = held.at[0], held.at[1]
    lost = n_blocks - slots
    pieces = lost * 2
    row = lax.broadcasted_iota(jnp.int32, (16, kn_ref.shape[1]), 0)

    def owned(b):
        p = pos_ref[b]
        return p, jnp.logical_and(p >= 0, p < seq_local)

    def keep_copies(t):
        s = lax.rem(t, slots)
        rows = pl.ds(t * nh, nh)
        return (pltpu.make_async_copy(kr.at[s], ko_hbm.at[rows], sem_keep.at[0, s]),
                pltpu.make_async_copy(vr.at[s], vo_hbm.at[rows], sem_keep.at[1, s]))

    def in_copies(j):
        rows = pl.ds(j * step, step)
        return (pltpu.make_async_copy(k_hbm.at[rows], kc.at[lax.rem(j, 2)], sem_in.at[0, lax.rem(j, 2)]),
                pltpu.make_async_copy(v_hbm.at[rows], vc.at[lax.rem(j, 2)], sem_in.at[1, lax.rem(j, 2)]))

    def out_copies(j):
        rows = pl.ds(j * step, step)
        return (pltpu.make_async_copy(kc.at[lax.rem(j, 2)], ko_hbm.at[rows], sem_out.at[0, lax.rem(j, 2)]),
                pltpu.make_async_copy(vc.at[lax.rem(j, 2)], vo_hbm.at[rows], sem_out.at[1, lax.rem(j, 2)]))

    def fixed(src, new_ref, b, base, p):
        return jnp.where(row + base == p, new_ref[b].astype(BF16), src)

    for j in range(min(2, pieces)):
        for cp in in_copies(j):
            cp.start()

    def begin(t, c):
        for cp in keep_copies(t):
            cp.start()
        return c

    lax.fori_loop(lost, n_blocks, begin, 0)

    def again(j, c):
        for cp in in_copies(j):
            cp.wait()
        for i in range(step):
            b = j * step + i
            p, own = owned(b)

            @pl.when(own)
            def _():
                base = pl.multiple_of(p // 16 * 16, 16)
                for buf, new_ref in ((kc, kn_ref), (vc, vn_ref)):
                    at = (lax.rem(j, 2), i, pl.ds(base, 16), slice(None))
                    buf[at] = fixed(buf[at], new_ref, b, base, p)
        for cp in out_copies(j):
            cp.start()

        @pl.when(j + 2 < pieces)
        def _():
            for cp in out_copies(j):
                cp.wait()
            for cp in in_copies(j + 2):
                cp.start()
        return c

    lax.fori_loop(0, pieces, again, 0)

    def slab(b, c):
        p, own = owned(b)

        @pl.when(own)
        def _():
            t = b // nh
            base = pl.multiple_of(p // 16 * 16, 16)
            at = (lax.rem(t, slots), lax.rem(b, nh), pl.ds(base, 16), slice(None))
            k_slab[b - lost * nh] = fixed(kr[at], kn_ref, b, base, p)
            v_slab[b - lost * nh] = fixed(vr[at], vn_ref, b, base, p)
        return c

    lax.fori_loop(lost * nh, n_seq, slab, 0)

    def slab_copies(b, p):
        at = pl.ds(pl.multiple_of(p // 16 * 16, 16), 16)
        return (pltpu.make_async_copy(k_slab.at[b - lost * nh], ko_hbm.at[b, at], sem_slab.at[0]),
                pltpu.make_async_copy(v_slab.at[b - lost * nh], vo_hbm.at[b, at], sem_slab.at[1]))

    def patch(t, c):
        for cp in keep_copies(t):
            cp.wait()

        def one(i, c):
            p, own = owned(t * nh + i)

            @pl.when(own)
            def _():
                for cp in slab_copies(t * nh + i, p):
                    cp.start()
            return c
        return lax.fori_loop(0, nh, one, c)

    lax.fori_loop(lost, n_blocks, patch, 0)

    def drain(b, c):
        p, own = owned(b)

        @pl.when(own)
        def _():
            for cp in slab_copies(b, p):
                cp.wait()
        return c

    lax.fori_loop(lost * nh, n_seq, drain, 0)
    for j in range(max(pieces - 2, 0), pieces):
        for cp in out_copies(j):
            cp.wait()


def solution(mesh):
    def local_step(tokens, w_query, w_key, w_value, w_out, k_cache, v_cache, positions):
        n_seq, seq_local, hd = k_cache.shape
        width = w_query.shape[1]
        heads = width // hd
        nh = HALF
        groups = n_seq // (2 * nh)
        n_blocks = 2 * groups
        slots = n_blocks * 3 // 4
        q = jnp.dot(tokens, w_query, preferred_element_type=F32).astype(BF16).reshape(n_seq, heads, hd)
        k_new = jnp.dot(tokens, w_key, preferred_element_type=F32).astype(BF16).astype(F32)
        v_new = jnp.dot(tokens, w_value, preferred_element_type=F32).astype(BF16).astype(F32)
        local_pos = positions - lax.axis_index('sp') * seq_local
        vmem, hbm = pl.BlockSpec(memory_space=pltpu.VMEM), pl.BlockSpec(memory_space=pl.ANY)
        smem = pl.BlockSpec(memory_space=pltpu.SMEM)
        dma = pltpu.SemaphoreType.DMA
        held = pltpu.VMEM((2, slots, nh, seq_local, hd), BF16)
        rows_d, rows_1, quarter = heads * nh + heads, 2 * nh + heads, width // 4
        y, kept = pl.pallas_call(
            functools.partial(attend_kernel, (n_seq, heads, seq_local, hd, groups, slots)),
            out_shape=(jax.ShapeDtypeStruct((n_blocks, nh, width), BF16), held),
            in_specs=[smem, vmem, vmem, vmem, vmem, hbm, hbm],
            out_specs=(vmem, vmem),
            scratch_shapes=[
                pltpu.VMEM((groups, 2, 2, rows_d, 128), F32),
                pltpu.VMEM((groups, 2, rows_d, 128), F32),
                pltpu.VMEM((groups, 4, 2, rows_1, 128), F32),
                pltpu.VMEM((groups, 3, 2, rows_1, 128), F32),
                pltpu.VMEM((groups, 4, nh, quarter), F32),
                pltpu.VMEM((groups, 3, nh, quarter), F32),
                pltpu.VMEM((n_blocks, nh, width), BF16),
                pltpu.VMEM((2,) + w_out.shape, BF16),
                dma((slots,)), dma((slots,)), dma((3,)),
                dma((groups,)), dma((groups,)),
                dma((groups, 3)), dma((groups, 3)),
                dma((groups, 3)), dma((groups, 3)),
                dma((groups, 3)), dma((groups, 3)),
                dma((groups,)), dma((groups,)),
            ],
            compiler_params=pltpu.CompilerParams(collective_id=0, has_side_effects=True,
                                                 vmem_limit_bytes=VMEM_A),
        )(local_pos, q, k_new, v_new, w_out, k_cache, v_cache)
        keep = slots * nh
        k_upd, v_upd = pl.pallas_call(
            functools.partial(write_kernel, (n_seq, seq_local, n_blocks, slots)),
            out_shape=(jax.ShapeDtypeStruct(k_cache.shape, BF16),) * 2,
            in_specs=[smem, vmem, vmem, vmem, hbm, hbm],
            out_specs=(hbm, hbm),
            scratch_shapes=[
                pltpu.VMEM((2, nh // 2, seq_local, hd), BF16), pltpu.VMEM((2, nh // 2, seq_local, hd), BF16),
                pltpu.VMEM((keep, 16, hd), BF16), pltpu.VMEM((keep, 16, hd), BF16),
                dma((2, 2)), dma((2, 2)), dma((2, slots)), dma((2,)),
            ],
            compiler_params=pltpu.CompilerParams(vmem_limit_bytes=VMEM_B),
        )(local_pos, k_new.reshape(n_seq, 1, hd), v_new.reshape(n_seq, 1, hd),
          pltpu.with_memory_space_constraint(kept, pltpu.VMEM), k_cache, v_cache)
        return y.reshape(n_seq, width), k_upd, v_upd

    cache_spec = P('dp', 'sp', None)
    return jax.shard_map(local_step, mesh=mesh, in_specs=(P('dp', None), P(), P(), P(), P('sp', None), cache_spec, cache_spec, P('dp')), out_specs=(P('dp', None), cache_spec, cache_spec), check_vma=False)


VMEM_A = 14 << 20
VMEM_B = 8 << 20
```

time: 219 us -> 104 us (0.47)
  the two profiles are of different devices: /device:TPU:0 before, /device:TPU:5 now
where the time goes in v1:
time: 104 us; the launch traced here: 103 us
  Pallas kernels  86.9 us (84%)
  matrix products  9.12 us (9%)
  local copies, waits for them, and re-layouts  5.37 us (5%)
  other arithmetic  1.33 us (1%)
    pallas_call x1, Pallas kernels, local_step(): pl.pallas_call(functools.partial(attend_kernel, (n_seq, heads, seq_local,...  49.2 us
    pallas_call x1, Pallas kernels, local_step(): pl.pallas_call(functools.partial(write_kernel, (n_seq, seq_local, n_block...  37.8 us
    dot_general x1, matrix products, local_step(): jnp.dot(tokens, w_query, preferred_element_type=F32).astype(BF16)  5.71 us
    unnamed x10, local copies, waits for them, and re-layouts  3.61 us

profile of v1, /device:TPU:5, one launch (start us, length us, event | category | flops | bytes accessed | tf_op | source)
XLA Modules:
  0.0 103.5 jit_solution(14011206854278997390)
XLA Ops:
  0.6 0.0 copy-start
  0.7 1.3 %broadcast_subtract_fusion.pos_ref = s32[256]{0:T(256)} fusion(s32[256]{0:T(256)} %param.15, s32[]{:T(128)S(6)} %mul.3), kind=kLoop, calls=%fused_computation.5 | loop fusion | flops 256 | bytes 2052 | tf_op jit(solution)/shard_map/sub | solution.py:353
  2.0 0.0 copy-done
  2.0 1.7 %fusion.1.kn_ref = f32[256,256]{1,0:T(8,128)S(1)} fusion(bf16[256,2048]{1,0:T(8,128)(2,1)S(1)} %copy-done, bf16[2048,256]{1,0:T(8,128)(2,1)} %param.10), kind=kOutput, calls=%fused_computation.4 | convolution fusion | flops 268566528 | bytes 2359296 | tf_op jit(solution)/shard_map/dot_general | solution.py:351
  3.7 0.0 copy-start.2
  3.7 1.8 %fusion.vn_ref = f32[256,256]{1,0:T(8,128)S(1)} fusion(bf16[256,2048]{1,0:T(8,128)(2,1)S(1)} %copy-done, bf16[2048,256]{1,0:T(8,128)(2,1)} %param.11), kind=kOutput, calls=%fused_computation.2 | convolution fusion | flops 268566528 | bytes 2359296 | tf_op jit(solution)/shard_map/dot_general | solution.py:352
  5.4 0.0 copy-start.3
  5.4 0.9 reshape.21.vn_ref
  6.3 0.9 reshape.20.kn_ref
  7.2 5.7 %convolution_convert_fusion = bf16[256,2048]{1,0:T(8,128)(2,1)S(1)} fusion(bf16[256,2048]{1,0:T(8,128)(2,1)S(1)} %copy-done, bf16[2048,2048]{1,0:T(8,128)(2,1)} %param.9), kind=kOutput, calls=%fused_computation | convolution fusion | flops 2148007936 | bytes 10485760 | tf_op jit(solution)/shard_map/dot_general | solution.py:350
  12.9 1.3 %copy.11 = bf16[32,8,8,256]{3,2,1,0:T(8,128)(2,1)} copy(bf16[32,8,8,256]{3,1,2,0:T(8,128)(2,1)S(1)} %bitcast.11) | data formatting | bytes 2097152
  14.2 0.0 copy-done.2
  14.2 0.0 copy-done.3
  14.2 49.2 %shard_map.103 = (bf16[16,16,2048]{2,1,0:T(8,128)(2,1)}, bf16[2,12,16,256,256]{4,3,2,1,0:T(8,128)(2,1)S(1)}) custom-call(s32[256]{0:T(256)} %broadcast_subtract_fusion.pos_ref, bf16[256,8,256]{2,1,0:T(8,128)(2,1)} %bitcast.9, f32[256,256]{1,0:T(8,128)} %copy-done.2, f32[256,256]{1,0:T(8,128)} %copy-done.3, bf16[256,2048]{1,0:T(8,128)(2,1)} %wo_ref.1, ...), custom_call_target="tpu_custom_call" | custom-call | tf_op jit(solution)/shard_map/pallas_call | solution.py:359
  63.4 0.0 copy-start.1
  63.4 37.8 %shard_map.104 = (bf16[256,256,256]{2,1,0:T(8,128)(2,1)}, bf16[256,256,256]{2,1,0:T(8,128)(2,1)}) custom-call(s32[256]{0:T(256)} %broadcast_subtract_fusion.pos_ref, f32[256,1,256]{2,1,0:T(1,128)} %reshape.20.kn_ref, f32[256,1,256]{2,1,0:T(1,128)} %reshape.21.vn_ref, bf16[2,12,16,256,256]{4,3,2,1,0:T(8,128)(2,1)S(1)} %get-tuple-element.8.held, ...), custom_call_target="tpu_custom_call" | custom-call | tf_op jit(solution)/shard_map/pallas_call | solution.py:384
  101.2 2.3 %copy.13 = bf16[256,2048]{1,0:T(8,128)(2,1)} copy(bf16[256,2048]{1,0:T(8,128)(2,1)} %bitcast.10) | data formatting | bytes 2097152
  103.5 0.0 copy-done.1
Async XLA Ops:
  0.6 1.4 %copy-start = (bf16[256,2048]{1,0:T(8,128)(2,1)S(1)}, bf16[256,2048]{1,0:T(8,128)(2,1)}, u32[]{:S(2)}) copy-start(bf16[256,2048]{1,0:T(8,128)(2,1)} %param.8) | copy-start | bytes 3145732
  3.7 10.5 %copy-start.2 = (f32[256,256]{1,0:T(8,128)}, f32[256,256]{1,0:T(8,128)S(1)}, u32[]{:S(2)}) copy-start(f32[256,256]{1,0:T(8,128)S(1)} %fusion.1.kn_ref) | copy-start | bytes 786436
  5.4 8.8 %copy-start.3 = (f32[256,256]{1,0:T(8,128)}, f32[256,256]{1,0:T(8,128)S(1)}, u32[]{:S(2)}) copy-start(f32[256,256]{1,0:T(8,128)S(1)} %fusion.vn_ref) | copy-start | bytes 786436
  63.4 40.1 %copy-start.1 = (bf16[256,2048]{1,0:T(8,128)(2,1)S(1)}, bf16[256,2048]{1,0:T(8,128)(2,1)}, u32[]{:S(2)}) copy-start(bf16[256,2048]{1,0:T(8,128)(2,1)} %param.8) | copy-start | bytes 3145732

commit v2 on v1

--- a/solution.py
+++ b/solution.py
@@ -11,6 +11,7 @@
 F32, BF16 = jnp.float32, jnp.bfloat16
 FLOOR = -1e30
 HALF = 16
+RING = 4
 LAG_C, LAG_S, LAG_R = 3, 5, 7
 
 
@@ -85,7 +86,7 @@
         for cp in cache_copies(t):
             cp.wait()
         first = pl.multiple_of(t * nh, nh)
-        kn, vn = kn_ref[pl.ds(first, nh), :], vn_ref[pl.ds(first, nh), :]
+        kn, vn = kn_ref[pl.ds(first, nh), :].astype(F32), vn_ref[pl.ds(first, nh), :].astype(F32)
         scores = []
         for i in range(nh):
             scores.append(lax.dot_general(q_ref[first + i], kb[s, i], (((1,), (1,)), ((), ())),
@@ -218,124 +219,75 @@
     y_ref[...] = ybuf[...]
 
 
-def write_kernel(dims, pos_ref, kn_ref, vn_ref, held, k_hbm, v_hbm, ko_hbm, vo_hbm,
-                 kc, vc, k_slab, v_slab, sem_in, sem_out, sem_keep, sem_slab):
+def write_kernel(dims, pos_ref, kn_ref, vn_ref, y_in, _, k_hbm, v_hbm, ko_hbm, vo_hbm, y_hbm, held,
+                 kc, vc, sem_in, sem_out, sem_keep, sem_y):
     n_seq, seq_local, n_blocks, slots = dims
     nh = HALF
     step = nh // 2
-    kr, vr = held.at[0], held.at[1]
     lost = n_blocks - slots
     pieces = lost * 2
-    row = lax.broadcasted_iota(jnp.int32, (16, kn_ref.shape[1]), 0)
-
-    def owned(b):
-        p = pos_ref[b]
-        return p, jnp.logical_and(p >= 0, p < seq_local)
+    row = lax.broadcasted_iota(jnp.int32, (16, kn_ref.shape[-1]), 0)
 
     def keep_copies(t):
-        s = lax.rem(t, slots)
+        s = t % slots
         rows = pl.ds(t * nh, nh)
-        return (pltpu.make_async_copy(kr.at[s], ko_hbm.at[rows], sem_keep.at[0, s]),
-                pltpu.make_async_copy(vr.at[s], vo_hbm.at[rows], sem_keep.at[1, s]))
+        return (pltpu.make_async_copy(held.at[0, s], ko_hbm.at[rows], sem_keep.at[0, s]),
+                pltpu.make_async_copy(held.at[1, s], vo_hbm.at[rows], sem_keep.at[1, s]))
 
     def in_copies(j):
-        rows = pl.ds(j * step, step)
-        return (pltpu.make_async_copy(k_hbm.at[rows], kc.at[lax.rem(j, 2)], sem_in.at[0, lax.rem(j, 2)]),
-                pltpu.make_async_copy(v_hbm.at[rows], vc.at[lax.rem(j, 2)], sem_in.at[1, lax.rem(j, 2)]))
+        rows, r = pl.ds(j * step, step), j % RING
+        return (pltpu.make_async_copy(k_hbm.at[rows], kc.at[r], sem_in.at[0, r]),
+                pltpu.make_async_copy(v_hbm.at[rows], vc.at[r], sem_in.at[1, r]))
 
     def out_copies(j):
-        rows = pl.ds(j * step, step)
-        return (pltpu.make_async_copy(kc.at[lax.rem(j, 2)], ko_hbm.at[rows], sem_out.at[0, lax.rem(j, 2)]),
-                pltpu.make_async_copy(vc.at[lax.rem(j, 2)], vo_hbm.at[rows], sem_out.at[1, lax.rem(j, 2)]))
-
-    def fixed(src, new_ref, b, base, p):
-        return jnp.where(row + base == p, new_ref[b].astype(BF16), src)
-
-    for j in range(min(2, pieces)):
-        for cp in in_copies(j):
+        rows, r = pl.ds(j * step, step), j % RING
+        return (pltpu.make_async_copy(kc.at[r], ko_hbm.at[rows], sem_out.at[0, r]),
+                pltpu.make_async_copy(vc.at[r], vo_hbm.at[rows], sem_out.at[1, r]))
+
+    def start(copies):
+        for cp in copies:
             cp.start()
 
-    def begin(t, c):
-        for cp in keep_copies(t):
-            cp.start()
-        return c
-
-    lax.fori_loop(lost, n_blocks, begin, 0)
-
-    def again(j, c):
-        for cp in in_copies(j):
+    def wait(copies):
+        for cp in copies:
             cp.wait()
-        for i in range(step):
-            b = j * step + i
-            p, own = owned(b)
-
-            @pl.when(own)
+
+    def renew(bufs, first, n):
+        def one(i, c):
+            p = pos_ref[first + i]
+
+            @pl.when(jnp.logical_and(p >= 0, p < seq_local))
             def _():
                 base = pl.multiple_of(p // 16 * 16, 16)
-                for buf, new_ref in ((kc, kn_ref), (vc, vn_ref)):
-                    at = (lax.rem(j, 2), i, pl.ds(base, 16), slice(None))
-                    buf[at] = fixed(buf[at], new_ref, b, base, p)
-        for cp in out_copies(j):
-            cp.start()
-
-        @pl.when(j + 2 < pieces)
-        def _():
-            for cp in out_copies(j):
-                cp.wait()
-            for cp in in_copies(j + 2):
-                cp.start()
-        return c
-
-    lax.fori_loop(0, pieces, again, 0)
-
-    def slab(b, c):
-        p, own = owned(b)
-
-        @pl.when(own)
-        def _():
-            t = b // nh
-            base = pl.multiple_of(p // 16 * 16, 16)
-            at = (lax.rem(t, slots), lax.rem(b, nh), pl.ds(base, 16), slice(None))
-            k_slab[b - lost * nh] = fixed(kr[at], kn_ref, b, base, p)
-            v_slab[b - lost * nh] = fixed(vr[at], vn_ref, b, base, p)
-        return c
-
-    lax.fori_loop(lost * nh, n_seq, slab, 0)
-
-    def slab_copies(b, p):
-        at = pl.ds(pl.multiple_of(p // 16 * 16, 16), 16)
-        return (pltpu.make_async_copy(k_slab.at[b - lost * nh], ko_hbm.at[b, at], sem_slab.at[0]),
-                pltpu.make_async_copy(v_slab.at[b - lost * nh], vo_hbm.at[b, at], sem_slab.at[1]))
-
-    def patch(t, c):
-        for cp in keep_copies(t):
-            cp.wait()
-
-        def one(i, c):
-            p, own = owned(t * nh + i)
-
-            @pl.when(own)
-            def _():
-                for cp in slab_copies(t * nh + i, p):
-                    cp.start()
+                for buf, new_ref in zip(bufs, (kn_ref, vn_ref)):
+                    at = (i, pl.ds(base, 16), slice(None))
+                    buf[at] = jnp.where(row + base == p, new_ref[first + i].astype(BF16), buf[at])
             return c
-        return lax.fori_loop(0, nh, one, c)
-
-    lax.fori_loop(lost, n_blocks, patch, 0)
-
-    def drain(b, c):
-        p, own = owned(b)
-
-        @pl.when(own)
-        def _():
-            for cp in slab_copies(b, p):
-                cp.wait()
-        return c
-
-    lax.fori_loop(lost * nh, n_seq, drain, 0)
-    for j in range(max(pieces - 2, 0), pieces):
-        for cp in out_copies(j):
-            cp.wait()
+        lax.fori_loop(0, n, one, 0)
+
+    y_copy = pltpu.make_async_copy(y_in, y_hbm, sem_y)
+    y_copy.start()
+    for j in range(min(RING, pieces)):
+        start(in_copies(j))
+    done = 0
+    for j in range(pieces):
+        upto = slots * (j + 1) // pieces
+        for t in range(lost + done, lost + upto):
+            renew((held.at[0, t % slots], held.at[1, t % slots]), t * nh, nh)
+        for t in range(lost + done, lost + upto):
+            start(keep_copies(t))
+        done = upto
+        if 1 <= j and j - 1 + RING < pieces:
+            wait(out_copies(j - 1))
+            start(in_copies(j - 1 + RING))
+        wait(in_copies(j))
+        renew((kc.at[j % RING], vc.at[j % RING]), j * step, step)
+        start(out_copies(j))
+    for j in range(max(pieces - RING, 0), pieces):
+        wait(out_copies(j))
+    for t in range(lost, n_blocks):
+        wait(keep_copies(t))
+    y_copy.wait()
 
 
 def solution(mesh):
@@ -348,8 +300,8 @@
         n_blocks = 2 * groups
         slots = n_blocks * 3 // 4
         q = jnp.dot(tokens, w_query, preferred_element_type=F32).astype(BF16).reshape(n_seq, heads, hd)
-        k_new = jnp.dot(tokens, w_key, preferred_element_type=F32).astype(BF16).astype(F32)
-        v_new = jnp.dot(tokens, w_value, preferred_element_type=F32).astype(BF16).astype(F32)
+        k_new = jnp.dot(tokens, w_key, preferred_element_type=F32).astype(BF16)
+        v_new = jnp.dot(tokens, w_value, preferred_element_type=F32).astype(BF16)
         local_pos = positions - lax.axis_index('sp') * seq_local
         vmem, hbm = pl.BlockSpec(memory_space=pltpu.VMEM), pl.BlockSpec(memory_space=pl.ANY)
         smem = pl.BlockSpec(memory_space=pltpu.SMEM)
@@ -380,19 +332,18 @@
             compiler_params=pltpu.CompilerParams(collective_id=0, has_side_effects=True,
                                                  vmem_limit_bytes=VMEM_A),
         )(local_pos, q, k_new, v_new, w_out, k_cache, v_cache)
-        keep = slots * nh
-        k_upd, v_upd = pl.pallas_call(
+        k_upd, v_upd, y, _ = pl.pallas_call(
             functools.partial(write_kernel, (n_seq, seq_local, n_blocks, slots)),
-            out_shape=(jax.ShapeDtypeStruct(k_cache.shape, BF16),) * 2,
-            in_specs=[smem, vmem, vmem, vmem, hbm, hbm],
-            out_specs=(hbm, hbm),
+            out_shape=(jax.ShapeDtypeStruct(k_cache.shape, BF16),) * 2 + (jax.ShapeDtypeStruct(y.shape, BF16), held),
+            in_specs=[smem, vmem, vmem, vmem, vmem, hbm, hbm],
+            out_specs=(hbm, hbm, hbm, vmem),
+            input_output_aliases={4: 3},
             scratch_shapes=[
-                pltpu.VMEM((2, nh // 2, seq_local, hd), BF16), pltpu.VMEM((2, nh // 2, seq_local, hd), BF16),
-                pltpu.VMEM((keep, 16, hd), BF16), pltpu.VMEM((keep, 16, hd), BF16),
-                dma((2, 2)), dma((2, 2)), dma((2, slots)), dma((2,)),
+                pltpu.VMEM((RING, nh // 2, seq_local, hd), BF16), pltpu.VMEM((RING, nh // 2, seq_local, hd), BF16),
+                dma((2, RING)), dma((2, RING)), dma((2, slots)), dma,
             ],
             compiler_params=pltpu.CompilerParams(vmem_limit_bytes=VMEM_B),
-        )(local_pos, k_new.reshape(n_seq, 1, hd), v_new.reshape(n_seq, 1, hd),
+        )(local_pos, k_new.astype(F32).reshape(n_seq, 1, hd), v_new.astype(F32).reshape(n_seq, 1, hd), y,
           pltpu.with_memory_space_constraint(kept, pltpu.VMEM), k_cache, v_cache)
         return y.reshape(n_seq, width), k_upd, v_upd
 
@@ -401,4 +352,4 @@
 
 
 VMEM_A = 14 << 20
-VMEM_B = 8 << 20
+VMEM_B = 12 << 20

time: 104 us -> 93.7 us (0.901)
  the two profiles are of different devices: /device:TPU:5 before, /device:TPU:0 now
where the time goes in v2:
time: 93.7 us; the launch traced here: 93.4 us
  Pallas kernels  79.3 us (85%)
  matrix products  9.08 us (10%)
  local copies, waits for them, and re-layouts  2.98 us (3%)
  other arithmetic  1.33 us (1%)
    pallas_call x1, Pallas kernels, local_step(): pl.pallas_call(functools.partial(attend_kernel, (n_seq, heads, seq_local,...  50.7 us
    pallas_call x1, Pallas kernels, local_step(): pl.pallas_call(functools.partial(write_kernel, (n_seq, seq_local, n_block...  28.6 us
    dot_general x1, matrix products, local_step(): jnp.dot(tokens, w_query, preferred_element_type=F32).astype(BF16)  5.71 us

profile of v2, /device:TPU:0, one launch (start us, length us, event | category | flops | bytes accessed | tf_op | source)
XLA Modules:
  0.0 93.4 jit_solution(10907651866253685731)
XLA Ops:
  0.6 0.0 copy-start
  0.7 1.3 %broadcast_subtract_fusion.pos_ref = s32[256]{0:T(256)} fusion(s32[256]{0:T(256)} %param.15, s32[]{:T(128)S(6)} %mul.3), kind=kLoop, calls=%fused_computation.3 | loop fusion | flops 256 | bytes 2052 | tf_op jit(solution)/shard_map/sub | solution.py:305
  2.0 0.0 copy-done
  2.0 1.7 %convolution_convert_fusion.2.kn_ref = bf16[256,256]{1,0:T(8,128)(2,1)S(1)} fusion(bf16[256,2048]{1,0:T(8,128)(2,1)S(1)} %copy-done, bf16[2048,256]{1,0:T(8,128)(2,1)} %param.10), kind=kOutput, calls=%fused_computation.2 | convolution fusion | flops 268500992 | bytes 2228224 | tf_op jit(solution)/shard_map/dot_general | solution.py:303
  3.7 0.0 copy-start.2
  3.7 1.7 %convolution_convert_fusion.1.vn_ref = bf16[256,256]{1,0:T(8,128)(2,1)S(1)} fusion(bf16[256,2048]{1,0:T(8,128)(2,1)S(1)} %copy-done, bf16[2048,256]{1,0:T(8,128)(2,1)} %param.11), kind=kOutput, calls=%fused_computation.1 | convolution fusion | flops 268500992 | bytes 2228224 | tf_op jit(solution)/shard_map/dot_general | solution.py:304
  5.4 0.0 copy-start.3
  5.4 0.8 reshape.31.vn_ref
  6.2 0.8 reshape.29.kn_ref
  7.1 5.7 %convolution_convert_fusion = bf16[256,2048]{1,0:T(8,128)(2,1)S(1)} fusion(bf16[256,2048]{1,0:T(8,128)(2,1)S(1)} %copy-done, bf16[2048,2048]{1,0:T(8,128)(2,1)} %param.9), kind=kOutput, calls=%fused_computation | convolution fusion | flops 2148007936 | bytes 10485760 | tf_op jit(solution)/shard_map/dot_general | solution.py:302
  12.8 1.3 %copy.12 = bf16[32,8,8,256]{3,2,1,0:T(8,128)(2,1)} copy(bf16[32,8,8,256]{3,1,2,0:T(8,128)(2,1)S(1)} %bitcast.10) | data formatting | bytes 2097152
  14.1 0.0 copy-done.2
  14.1 0.0 copy-done.3
  14.1 50.7 %shard_map.103 = (bf16[16,16,2048]{2,1,0:T(8,128)(2,1)}, bf16[2,12,16,256,256]{4,3,2,1,0:T(8,128)(2,1)S(1)}) custom-call(s32[256]{0:T(256)} %broadcast_subtract_fusion.pos_ref, bf16[256,8,256]{2,1,0:T(8,128)(2,1)} %bitcast.9, bf16[256,256]{1,0:T(8,128)(2,1)} %copy-done.2, bf16[256,256]{1,0:T(8,128)(2,1)} %copy-done.3, bf16[256,2048]{1,0:T(8,128)(2,1)} %wo_ref.1, ...), custom_call_target="tpu_custom_call" | custom-call | tf_op jit(solution)/shard_map/pallas_call | solution.py:311
  64.8 0.0 copy-start.1
  64.8 28.6 %shard_map.104 = (bf16[256,256,256]{2,1,0:T(8,128)(2,1)}, bf16[256,256,256]{2,1,0:T(8,128)(2,1)}, bf16[16,16,2048]{2,1,0:T(8,128)(2,1)}, bf16[2,12,16,256,256]{4,3,2,1,0:T(8,128)(2,1)S(1)}) custom-call(s32[256]{0:T(256)} %broadcast_subtract_fusion.pos_ref, f32[256,1,256]{2,1,0:T(1,128)} %reshape.29.kn_ref, ...), custom_call_target="tpu_custom_call", output_to_operand_aliasing={{3}: (4, {})} | custom-call | tf_op jit(solution)/shard_map/pallas_call | solution.py:335
  93.4 0.0 copy-done.1
Async XLA Ops:
  0.6 1.4 %copy-start = (bf16[256,2048]{1,0:T(8,128)(2,1)S(1)}, bf16[256,2048]{1,0:T(8,128)(2,1)}, u32[]{:S(2)}) copy-start(bf16[256,2048]{1,0:T(8,128)(2,1)} %param.8) | copy-start | bytes 3145732
  3.7 10.4 %copy-start.2 = (bf16[256,256]{1,0:T(8,128)(2,1)}, bf16[256,256]{1,0:T(8,128)(2,1)S(1)}, u32[]{:S(2)}) copy-start(bf16[256,256]{1,0:T(8,128)(2,1)S(1)} %convolution_convert_fusion.2.kn_ref) | copy-start | bytes 393220
  5.4 8.7 %copy-start.3 = (bf16[256,256]{1,0:T(8,128)(2,1)}, bf16[256,256]{1,0:T(8,128)(2,1)S(1)}, u32[]{:S(2)}) copy-start(bf16[256,256]{1,0:T(8,128)(2,1)S(1)} %convolution_convert_fusion.1.vn_ref) | copy-start | bytes 393220
  64.8 28.7 %copy-start.1 = (bf16[256,2048]{1,0:T(8,128)(2,1)S(1)}, bf16[256,2048]{1,0:T(8,128)(2,1)}, u32[]{:S(2)}) copy-start(bf16[256,2048]{1,0:T(8,128)(2,1)} %param.8) | copy-start | bytes 3145732

commit v3 on v2

v3 whole, which is shorter than its diff:
```python
import functools

import jax
import jax.numpy as jnp
from jax import lax
from jax.experimental import pallas as pl
from jax.experimental.pallas import tpu as pltpu
from jax.sharding import PartitionSpec as P

MESH = pl.DeviceIdType.MESH
F32, BF16 = jnp.float32, jnp.bfloat16
FLOOR = -1e30
HALF = 16
RING = 4
LAG_C, LAG_S, LAG_R = 3, 5, 7


def attend_kernel(dims, pos_ref, x_ref, wq_hbm, wk_hbm, wv_hbm, wo_hbm, k_hbm, v_hbm,
                  y_ref, held, kn_ref, vn_ref,
                  q_ref, part, got_d, mix, got_1, obuf, wcol, sem_k, sem_v, sem_w, snd_w, rcv_w, snd_v, rcv_v,
                  snd_d, rcv_d, snd_1, rcv_1, snd_2, rcv_2, snd_3, rcv_3, snd_r, rcv_r):
    heads, seq_local, hd, groups, slots = dims
    nh = HALF
    width = wo_hbm.shape[1]
    n_blocks, quarter = 2 * groups, width // 4
    body = heads * nh
    scale = hd ** -0.5
    me = lax.axis_index('sp')
    chip, core = me // 2, lax.rem(me, 2)
    kb, vb = held.at[0], held.at[1]
    n_tiles = heads + 2
    first_stage = slots - pl.cdiv(n_tiles, 4)

    def peer(k):
        return {'sp': jnp.bitwise_xor(me, k)}

    def remote(src, dst, snd, rcv, k):
        return pltpu.make_async_remote_copy(src, dst, snd, rcv, device_id=peer(k), device_id_type=MESH)

    def columns(c):
        return pl.ds(pl.multiple_of(c * quarter, quarter), quarter)

    def cache_copies(t):
        s = lax.rem(t, slots)
        rows = pl.ds(t * nh, nh)
        return (pltpu.make_async_copy(k_hbm.at[rows], kb.at[s], sem_k.at[s]),
                pltpu.make_async_copy(v_hbm.at[rows], vb.at[s], sem_v.at[s]))

    def load(t):
        for cp in cache_copies(t):
            cp.start()

    def staged(w):
        return held.at[lax.rem(w, 4) // 2, first_stage + w // 4, pl.ds(lax.rem(w, 2) * 8, 8)]

    for w in range(n_tiles):
        src = wq_hbm.at[:, :, pl.ds(w * hd, hd)] if w < heads else (wk_hbm, wv_hbm)[w - heads]
        pltpu.make_async_copy(src, staged(w), sem_w.at[w]).start()

    gate = pltpu.get_barrier_semaphore()
    for k in (1, 2, 4, 6):
        pl.semaphore_signal(gate, inc=1, device_id=peer(k), device_id_type=MESH)
    pl.semaphore_wait(gate, 4)

    own_w = pltpu.make_async_copy(wo_hbm.at[:, columns(chip)], wcol.at[me], sem_w.at[n_tiles])

    def cross_w(k):
        return remote(wo_hbm.at[:, columns(jnp.bitwise_xor(chip, k))], wcol.at[me],
                      snd_w.at[k - 1], rcv_w.at[k - 1], 2 * k)

    def relay_w(k):
        src = jnp.bitwise_xor(me, 2 * k)
        return remote(wcol.at[src], wcol.at[src], snd_v.at[k], rcv_v.at[k], 1)

    for k in (3, 1, 2):
        cross_w(k).start()
    own_w.start()

    def d_copy(g):
        return remote(part.at[g, 1 - core], got_d.at[g], snd_d.at[g], rcv_d.at[g], 1)

    def one_copy(g, k):
        return remote(mix.at[g, jnp.bitwise_xor(chip, k)], got_1.at[g, k - 1],
                      snd_1.at[g, k - 1], rcv_1.at[g, k - 1], 2 * k)

    def two_copy(g, k):
        block = obuf.at[g, :, columns(chip)]
        return remote(block, block, snd_2.at[g, k - 1], rcv_2.at[g, k - 1], 2 * k)

    def three_copy(g, k):
        block = y_ref.at[2 * g + core, :, columns(chip)]
        return remote(block, block, snd_3.at[g, k - 1], rcv_3.at[g, k - 1], 2 * k)

    def relay_copy(g):
        rows = y_ref.at[2 * g + core]
        return remote(rows, rows, snd_r.at[g], rcv_r.at[g], 1)

    def tile(w, c):
        pltpu.make_async_copy(wk_hbm, staged(w), sem_w.at[w]).wait()

        @pl.when(w < first_stage)
        def _():
            load(w)
        wt = staged(w)[...].reshape(x_ref.shape[1], hd)
        acc = jnp.dot(x_ref[...], wt, preferred_element_type=F32)

        @pl.when(w < heads)
        def _():
            for z in range(2):
                q_ref[z, pl.ds(w, x_ref.shape[0], stride=heads), :] = acc[:, z * 128:(z + 1) * 128]

        @pl.when(w == heads)
        def _():
            kn_ref[...] = acc.astype(BF16).astype(F32)

        @pl.when(w == heads + 1)
        def _():
            vn_ref[...] = acc.astype(BF16).astype(F32)
        return c

    lax.fori_loop(0, n_tiles, tile, 0)
    for t in range(min(first_stage, n_tiles), slots):
        load(t)

    slot_ids = lax.broadcasted_iota(jnp.int32, (heads, seq_local), 1)
    lane = lax.broadcasted_iota(jnp.int32, (heads, 128), 1)

    def attend(g, half):
        t = 2 * g + half
        s = lax.rem(t, slots)
        for cp in cache_copies(t):
            cp.wait()
        first = pl.multiple_of(t * nh, nh)
        kn, vn = kn_ref[pl.ds(first, nh), :], vn_ref[pl.ds(first, nh), :]
        scores, qs = [], []
        for i in range(nh):
            rows = pl.ds(pl.multiple_of((first + i) * heads, heads), heads)
            q = jnp.concatenate([q_ref[0, rows, :], q_ref[1, rows, :]], axis=1).astype(BF16)
            qs.append(q)
            scores.append(lax.dot_general(q, kb[s, i], (((1,), (1,)), ((), ())), preferred_element_type=F32) * scale)
        peaks = jnp.full((heads, 128), FLOOR, F32)
        sums = jnp.zeros((heads, 128), F32)
        weights = []
        for i in range(nh):
            p = pos_ref[first + i] - me * seq_local
            own = jnp.logical_and(p >= 0, p < seq_local)
            sc = jnp.where(slot_ids < p, scores[i], -jnp.inf)
            fresh = jnp.sum(qs[i].astype(F32) * kn[i:i + 1, :], axis=1, keepdims=True) * scale
            fresh = jnp.where(own, fresh, -jnp.inf)
            m = jnp.maximum(jnp.maximum(jnp.max(sc, axis=1, keepdims=True), fresh), FLOOR)
            w, wf = jnp.exp(sc - m), jnp.exp(fresh - m)
            peaks = jnp.where(lane == i, m, peaks)
            sums = jnp.where(lane == i, jnp.sum(w, axis=1, keepdims=True) + wf, sums)
            weights.append((w.astype(BF16), wf.astype(BF16).astype(F32)))
        for i in range(nh):
            w, wf = weights[i]
            o = jnp.dot(w, vb[s, i], preferred_element_type=F32) + wf * vn[i:i + 1, :]
            for z in range(2):
                part[g, half, z, pl.ds(i, heads, stride=nh), :] = o[:, z * 128:(z + 1) * 128]
        part[g, half, 0, body:body + heads, :] = peaks
        part[g, half, 1, body:body + heads, :] = sums

        @pl.when(t + slots < n_blocks)
        def _():
            load(t + slots)

    def merge(g):
        d_copy(g).wait_recv()
        a, b = part.at[g, core], got_d.at[g]
        tail = slice(body, body + heads)
        m = jnp.maximum(a[0, tail, :], b[0, tail, :])
        ea, eb = jnp.exp(a[0, tail, :] - m), jnp.exp(b[0, tail, :] - m)
        total = a[1, tail, :] * ea + b[1, tail, :] * eb
        cols = jnp.transpose(jnp.concatenate([ea, eb], axis=0))
        for h in range(heads):
            rows = slice(h * nh, (h + 1) * nh)
            ca = jnp.broadcast_to(cols[:nh, h:h + 1], (nh, 128))
            cb = jnp.broadcast_to(cols[:nh, heads + h:heads + h + 1], (nh, 128))
            for z in range(2):
                at = (2 * z + h % 2) * nh
                mix[g, h // 2, at:at + nh, :] = a[z, rows, :] * ca + b[z, rows, :] * cb
        for c in range(4):
            mine = slice(2 * c, 2 * c + 2)
            mix[g, c, 4 * nh:4 * nh + 8, :] = jnp.concatenate([m[mine], total[mine], m[:4]], axis=0)

    def combine(g):
        for k in (1, 2, 3):
            one_copy(g, k).wait_recv()
        parts = [mix.at[g, chip]] + [got_1.at[g, k] for k in range(3)]
        stats = [r[4 * nh:4 * nh + 8, :] for r in parts]
        m = functools.reduce(jnp.maximum, stats)
        es = [jnp.exp(x - m) for x in stats]
        total = sum(e * jnp.concatenate([x[2:], x[:2]], axis=0) for e, x in zip(es, stats))
        total = jnp.where(total > 0, total, 1.0)
        cols = jnp.transpose(jnp.concatenate([e / total for e in es], axis=0))
        outs = []
        for j in range(2):
            cs = [jnp.broadcast_to(cols[:nh, i * 8 + j:i * 8 + j + 1], (nh, 128)) for i in range(4)]
            for z in range(2):
                at = (2 * z + j) * nh
                outs.append(sum(r[at:at + nh, :] * c for r, c in zip(parts, cs)))
        obuf[g, :, columns(chip)] = jnp.concatenate(outs, axis=1).astype(BF16)

    def project(g):
        for k in (1, 2, 3):
            two_copy(g, k).wait_recv()
        y = jnp.dot(obuf[g], wcol[...].reshape(width, quarter), preferred_element_type=F32)
        y_ref[2 * g + core, :, columns(chip)] = y.astype(BF16)

    def step(it, carry):
        @pl.when(it < groups)
        def _():
            lax.fori_loop(0, 2, lambda half, c: (attend(it, half), c)[1], 0)
            d_copy(it).start()

        @pl.when(it == LAG_C)
        def _():
            own_w.wait()
            relay_w(0).start()
            for k in (1, 2, 3):
                cross_w(k).wait()
                relay_w(k).start()

        @pl.when(jnp.logical_and(it >= 1, it < groups + 1))
        def _():
            merge(it - 1)
            for k in (3, 1, 2):
                one_copy(it - 1, k).start()

        @pl.when(jnp.logical_and(it >= LAG_C, it < groups + LAG_C))
        def _():
            combine(it - LAG_C)
            for k in (3, 1, 2):
                two_copy(it - LAG_C, k).start()

        @pl.when(it == LAG_S)
        def _():
            for k in range(4):
                relay_w(k).wait()

        @pl.when(jnp.logical_and(it >= LAG_S, it < groups + LAG_S))
        def _():
            project(it - LAG_S)
            for k in (3, 1, 2):
                three_copy(it - LAG_S, k).start()

        @pl.when(it >= LAG_R)
        def _():
            for k in (1, 2, 3):
                three_copy(it - LAG_R, k).wait_recv()
            relay_copy(it - LAG_R).start()
        return carry

    lax.fori_loop(0, groups + LAG_R, step, 0)

    def finish(g, carry):
        relay_copy(g).wait()
        d_copy(g).wait_send()
        for k in (1, 2, 3):
            one_copy(g, k).wait_send()
            two_copy(g, k).wait_send()
            three_copy(g, k).wait_send()
        return carry

    lax.fori_loop(0, groups, finish, 0)


def write_kernel(dims, pos_ref, kn_ref, vn_ref, y_in, _, k_hbm, v_hbm, ko_hbm, vo_hbm, y_hbm, held,
                 kc, vc, sem_in, sem_out, sem_keep, sem_y):
    n_seq, seq_local, n_blocks, slots = dims
    nh = HALF
    step = nh // 2
    lost = n_blocks - slots
    pieces = lost * 2
    row = lax.broadcasted_iota(jnp.int32, (16, kn_ref.shape[-1]), 0)

    def keep_copies(t):
        s = t % slots
        rows = pl.ds(t * nh, nh)
        return (pltpu.make_async_copy(held.at[0, s], ko_hbm.at[rows], sem_keep.at[0, s]),
                pltpu.make_async_copy(held.at[1, s], vo_hbm.at[rows], sem_keep.at[1, s]))

    def in_copies(j):
        rows, r = pl.ds(j * step, step), j % RING
        return (pltpu.make_async_copy(k_hbm.at[rows], kc.at[r], sem_in.at[0, r]),
                pltpu.make_async_copy(v_hbm.at[rows], vc.at[r], sem_in.at[1, r]))

    def out_copies(j):
        rows, r = pl.ds(j * step, step), j % RING
        return (pltpu.make_async_copy(kc.at[r], ko_hbm.at[rows], sem_out.at[0, r]),
                pltpu.make_async_copy(vc.at[r], vo_hbm.at[rows], sem_out.at[1, r]))

    def start(copies):
        for cp in copies:
            cp.start()

    def wait(copies):
        for cp in copies:
            cp.wait()

    def renew(bufs, first, n):
        def one(i, c):
            p = pos_ref[first + i] - lax.axis_index('sp') * seq_local

            @pl.when(jnp.logical_and(p >= 0, p < seq_local))
            def _():
                base = pl.multiple_of(p // 16 * 16, 16)
                around = pl.ds(pl.multiple_of((first + i) // 8 * 8, 8), 8)
                for buf, new_ref in zip(bufs, (kn_ref, vn_ref)):
                    at = (i, pl.ds(base, 16), slice(None))
                    new = jnp.sum(jnp.where(row[:8] == lax.rem(first + i, 8), new_ref[around, :], 0.0), axis=0, keepdims=True)
                    buf[at] = jnp.where(row + base == p, new.astype(BF16), buf[at])
            return c
        lax.fori_loop(0, n, one, 0)

    y_copy = pltpu.make_async_copy(y_in, y_hbm, sem_y)
    y_copy.start()
    for j in range(min(RING, pieces)):
        start(in_copies(j))
    done = 0
    for j in range(pieces):
        upto = slots * (j + 1) // pieces
        for t in range(lost + done, lost + upto):
            renew((held.at[0, t % slots], held.at[1, t % slots]), t * nh, nh)
        for t in range(lost + done, lost + upto):
            start(keep_copies(t))
        done = upto
        if 1 <= j and j - 1 + RING < pieces:
            wait(out_copies(j - 1))
            start(in_copies(j - 1 + RING))
        wait(in_copies(j))
        renew((kc.at[j % RING], vc.at[j % RING]), j * step, step)
        start(out_copies(j))
    for j in range(max(pieces - RING, 0), pieces):
        wait(out_copies(j))
    for t in range(lost, n_blocks):
        wait(keep_copies(t))
    y_copy.wait()


def solution(mesh):
    def local_step(tokens, w_query, w_key, w_value, w_out, k_cache, v_cache, positions):
        n_seq, seq_local, hd = k_cache.shape
        width = w_query.shape[1]
        heads = width // hd
        nh = HALF
        groups = n_seq // (2 * nh)
        n_blocks = 2 * groups
        slots = n_blocks * 3 // 4
        vmem, hbm = pl.BlockSpec(memory_space=pltpu.VMEM), pl.BlockSpec(memory_space=pl.ANY)
        smem = pl.BlockSpec(memory_space=pltpu.SMEM)
        dma = pltpu.SemaphoreType.DMA
        held = pltpu.VMEM((2, slots, nh, seq_local, hd), BF16)
        rows_d, rows_1 = heads * nh + heads, 4 * nh + 8
        d_model = tokens.shape[1]
        cut = d_model // 8
        n_stage = heads + 3
        y, kept, k_new, v_new = pl.pallas_call(
            functools.partial(attend_kernel, (heads, seq_local, hd, groups, slots)),
            out_shape=(jax.ShapeDtypeStruct((n_blocks, nh, width), BF16), held,
                       jax.ShapeDtypeStruct((n_seq, hd), F32), jax.ShapeDtypeStruct((n_seq, hd), F32)),
            in_specs=[smem, vmem, hbm, hbm, hbm, hbm, hbm, hbm],
            out_specs=(vmem,) * 4,
            scratch_shapes=[
                pltpu.VMEM((2, n_seq * heads, 128), F32),
                pltpu.VMEM((groups, 2, 2, rows_d, 128), F32),
                pltpu.VMEM((groups, 2, rows_d, 128), F32),
                pltpu.VMEM((groups, 4, rows_1, 128), F32),
                pltpu.VMEM((groups, 3, rows_1, 128), F32),
                pltpu.VMEM((groups, nh, width), BF16),
                pltpu.VMEM((heads, w_out.shape[0], width // 4), BF16),
                dma((slots,)), dma((slots,)), dma((n_stage,)),
                dma((3,)), dma((3,)), dma((4,)), dma((4,)),
                dma((groups,)), dma((groups,)),
                dma((groups, 3)), dma((groups, 3)),
                dma((groups, 3)), dma((groups, 3)),
                dma((groups, 3)), dma((groups, 3)),
                dma((groups,)), dma((groups,)),
            ],
            compiler_params=pltpu.CompilerParams(collective_id=0, has_side_effects=True,
                                                 vmem_limit_bytes=VMEM_A),
        )(positions, tokens, w_query.reshape(8, cut, width), w_key.reshape(8, cut, hd), w_value.reshape(8, cut, hd),
          w_out, k_cache, v_cache)
        kept = pltpu.with_memory_space_constraint(kept, pltpu.VMEM)
        k_upd, v_upd, y, _ = pl.pallas_call(
            functools.partial(write_kernel, (n_seq, seq_local, n_blocks, slots)),
            out_shape=(jax.ShapeDtypeStruct(k_cache.shape, BF16),) * 2 + (jax.ShapeDtypeStruct(y.shape, BF16), held),
            in_specs=[smem, vmem, vmem, vmem, vmem, hbm, hbm],
            out_specs=(hbm, hbm, hbm, vmem),
            input_output_aliases={4: 3},
            scratch_shapes=[
                pltpu.VMEM((RING, nh // 2, seq_local, hd), BF16), pltpu.VMEM((RING, nh // 2, seq_local, hd), BF16),
                dma((2, RING)), dma((2, RING)), dma((2, slots)), dma,
            ],
            compiler_params=pltpu.CompilerParams(vmem_limit_bytes=VMEM_B),
        )(positions, k_new, v_new, y, kept, k_cache, v_cache)
        return y.reshape(n_seq, width), k_upd, v_upd

    cache_spec = P('dp', 'sp', None)
    return jax.shard_map(local_step, mesh=mesh, in_specs=(P('dp', None), P(), P(), P(), P('sp', None), cache_spec, cache_spec, P('dp')), out_specs=(P('dp', None), cache_spec, cache_spec), check_vma=False)


VMEM_A = 14 << 20
VMEM_B = 12 << 20
```

time: 93.7 us -> 79.2 us (0.85)
  matrix products: 9.08 us -> 0 us
  local copies, waits for them, and re-layouts: 2.98 us -> 0 us
  other arithmetic: 1.33 us -> 0 us
  Pallas kernels: 79.3 us -> 78.3 us
    dot_general x3 -> x0, matrix products: 9.08 us -> none  [the longest x1 5.71 us: local_step(): jnp.dot(tokens, w_query, preferred_element_type=F32).astype(BF16)]
    reshape x2 -> x0, local copies, waits for them, and re-layouts: 1.67 us -> none  [the longest x1 0.84 us: local_step(): v_new.astype(F32).reshape(n_seq, 1, hd)]
    sub x1 -> x0, other arithmetic: 1.33 us -> none  [local_step(): local_pos = positions - lax.axis_index('sp') * seq_local]
    unnamed x9 -> x0, local copies, waits for them, and re-layouts: 1.31 us -> none
where the time goes in v3:
time: 79.2 us; the launch traced here: 79 us
  Pallas kernels  78.3 us (99%)
    pallas_call x1, Pallas kernels, local_step(): pl.pallas_call(functools.partial(attend_kernel, (heads, seq_local, hd, gr...  49.8 us
    pallas_call x1, Pallas kernels, local_step(): pl.pallas_call(functools.partial(write_kernel, (n_seq, seq_local, n_block...  28.6 us

profile of v3, /device:TPU:0, one launch (start us, length us, event | category | flops | bytes accessed | tf_op | source)
XLA Modules:
  0.0 79.0 jit_solution(12210481005047533447)
XLA Ops:
  0.6 49.8 %shard_map.103 = (bf16[16,16,2048]{2,1,0:T(8,128)(2,1)}, bf16[2,12,16,256,256]{4,3,2,1,0:T(8,128)(2,1)S(1)}, f32[256,256]{1,0:T(8,128)}, f32[256,256]{1,0:T(8,128)}) custom-call(s32[256]{0:T(256)} %pos_ref.3, bf16[256,2048]{1,0:T(8,128)(2,1)} %x_ref.1, bf16[8,256,2048]{2,1,0:T(8,128)(2,1)} %bitcast.4, bf16[8,256,256]{2,1,0:T(8,128)(2,1)} %bitcast.5, ...), custom_call_target="tpu_custom_call" | custom-call | tf_op jit(solution)/shard_map/pallas_call | solution.py:358
  50.4 28.6 %shard_map.104 = (bf16[256,256,256]{2,1,0:T(8,128)(2,1)}, bf16[256,256,256]{2,1,0:T(8,128)(2,1)}, bf16[16,16,2048]{2,1,0:T(8,128)(2,1)}, bf16[2,12,16,256,256]{4,3,2,1,0:T(8,128)(2,1)S(1)}) custom-call(s32[256]{0:T(256)} %pos_ref.3, f32[256,256]{1,0:T(8,128)} %get-tuple-element.10.kn_ref, ...), custom_call_target="tpu_custom_call", output_to_operand_aliasing={{3}: (4, {})} | custom-call | tf_op jit(solution)/shard_map/pallas_call | solution.py:385

commit v4 on v3

--- a/solution.py
+++ b/solution.py
@@ -12,13 +12,13 @@
 FLOOR = -1e30
 HALF = 16
 RING = 4
-LAG_C, LAG_S, LAG_R = 3, 5, 7
-
-
-def attend_kernel(dims, pos_ref, x_ref, wq_hbm, wk_hbm, wv_hbm, wo_hbm, k_hbm, v_hbm,
-                  y_ref, held, kn_ref, vn_ref,
-                  q_ref, part, got_d, mix, got_1, obuf, wcol, sem_k, sem_v, sem_w, snd_w, rcv_w, snd_v, rcv_v,
-                  snd_d, rcv_d, snd_1, rcv_1, snd_2, rcv_2, snd_3, rcv_3, snd_r, rcv_r):
+LAG_C, LAG_S, LAG_R, LAG_Y = 4, 7, 10, 12
+
+
+def attend_kernel(dims, pos_ref, x_hbm, wq_hbm, wk_hbm, wv_hbm, wo_hbm, k_hbm, v_hbm,
+                  y_hbm, held, kn_hbm, vn_hbm,
+                  x_ref, y_ref, kn_ref, vn_ref, q_ref, part, got_d, mix, got_1, obuf, wcol, sem_k, sem_v, sem_w, snd_w, rcv_w, snd_v, rcv_v,
+                  snd_d, rcv_d, snd_1, rcv_1, snd_2, rcv_2, snd_3, rcv_3, snd_r, rcv_r, sem_y):
     heads, seq_local, hd, groups, slots = dims
     nh = HALF
     width = wo_hbm.shape[1]
@@ -53,6 +53,8 @@
     def staged(w):
         return held.at[lax.rem(w, 4) // 2, first_stage + w // 4, pl.ds(lax.rem(w, 2) * 8, 8)]
 
+    x_copy = pltpu.make_async_copy(x_hbm, x_ref, sem_w.at[n_tiles + 1])
+    x_copy.start()
     for w in range(n_tiles):
         src = wq_hbm.at[:, :, pl.ds(w * hd, hd)] if w < heads else (wk_hbm, wv_hbm)[w - heads]
         pltpu.make_async_copy(src, staged(w), sem_w.at[w]).start()
@@ -95,6 +97,10 @@
         rows = y_ref.at[2 * g + core]
         return remote(rows, rows, snd_r.at[g], rcv_r.at[g], 1)
 
+    def y_copy(g):
+        rows = pl.ds(2 * g, 2)
+        return pltpu.make_async_copy(y_ref.at[rows], y_hbm.at[rows], sem_y.at[g])
+
     def tile(w, c):
         pltpu.make_async_copy(wk_hbm, staged(w), sem_w.at[w]).wait()
 
@@ -118,7 +124,10 @@
             vn_ref[...] = acc.astype(BF16).astype(F32)
         return c
 
+    x_copy.wait()
     lax.fori_loop(0, n_tiles, tile, 0)
+    kn_out = pltpu.make_async_copy(kn_ref, kn_hbm, sem_w.at[n_tiles])
+    vn_out = pltpu.make_async_copy(vn_ref, vn_hbm, sem_w.at[n_tiles + 1])
     for t in range(min(first_stage, n_tiles), slots):
         load(t)
 
@@ -216,6 +225,8 @@
         @pl.when(it == LAG_C)
         def _():
             own_w.wait()
+            kn_out.start()
+            vn_out.start()
             relay_w(0).start()
             for k in (1, 2, 3):
                 cross_w(k).wait()
@@ -244,17 +255,25 @@
             for k in (3, 1, 2):
                 three_copy(it - LAG_S, k).start()
 
-        @pl.when(it >= LAG_R)
+        @pl.when(jnp.logical_and(it >= LAG_R, it < groups + LAG_R))
         def _():
             for k in (1, 2, 3):
                 three_copy(it - LAG_R, k).wait_recv()
             relay_copy(it - LAG_R).start()
+
+        @pl.when(it >= LAG_Y)
+        def _():
+            relay_copy(it - LAG_Y).wait_recv()
+            y_copy(it - LAG_Y).start()
         return carry
 
-    lax.fori_loop(0, groups + LAG_R, step, 0)
+    lax.fori_loop(0, groups + LAG_Y, step, 0)
+    kn_out.wait()
+    vn_out.wait()
 
     def finish(g, carry):
-        relay_copy(g).wait()
+        relay_copy(g).wait_send()
+        y_copy(g).wait()
         d_copy(g).wait_send()
         for k in (1, 2, 3):
             one_copy(g, k).wait_send()
@@ -265,8 +284,8 @@
     lax.fori_loop(0, groups, finish, 0)
 
 
-def write_kernel(dims, pos_ref, kn_ref, vn_ref, y_in, _, k_hbm, v_hbm, ko_hbm, vo_hbm, y_hbm, held,
-                 kc, vc, sem_in, sem_out, sem_keep, sem_y):
+def write_kernel(dims, pos_ref, kn_hbm, vn_hbm, y_in, _, k_hbm, v_hbm, ko_hbm, vo_hbm, y_hbm, held,
+                 kn_ref, vn_ref, y_ref, kc, vc, sem_in, sem_out, sem_keep, sem_y):
     n_seq, seq_local, n_blocks, slots = dims
     nh = HALF
     step = nh // 2
@@ -313,10 +332,14 @@
             return c
         lax.fori_loop(0, n, one, 0)
 
-    y_copy = pltpu.make_async_copy(y_in, y_hbm, sem_y)
-    y_copy.start()
+    new_copies = (pltpu.make_async_copy(kn_hbm, kn_ref, sem_y.at[0]), pltpu.make_async_copy(vn_hbm, vn_ref, sem_y.at[1]))
+    start(new_copies)
     for j in range(min(RING, pieces)):
         start(in_copies(j))
+    y_take = pltpu.make_async_copy(y_in, y_ref, sem_y.at[2])
+    y_copy = pltpu.make_async_copy(y_ref, y_hbm, sem_y.at[2])
+    y_take.start()
+    wait(new_copies)
     done = 0
     for j in range(pieces):
         upto = slots * (j + 1) // pieces
@@ -331,6 +354,9 @@
         wait(in_copies(j))
         renew((kc.at[j % RING], vc.at[j % RING]), j * step, step)
         start(out_copies(j))
+        if j == pieces // 2:
+            y_take.wait()
+            y_copy.start()
     for j in range(max(pieces - RING, 0), pieces):
         wait(out_copies(j))
     for t in range(lost, n_blocks):
@@ -354,14 +380,16 @@
         rows_d, rows_1 = heads * nh + heads, 4 * nh + 8
         d_model = tokens.shape[1]
         cut = d_model // 8
-        n_stage = heads + 3
+        n_stage = heads + 4
         y, kept, k_new, v_new = pl.pallas_call(
             functools.partial(attend_kernel, (heads, seq_local, hd, groups, slots)),
             out_shape=(jax.ShapeDtypeStruct((n_blocks, nh, width), BF16), held,
                        jax.ShapeDtypeStruct((n_seq, hd), F32), jax.ShapeDtypeStruct((n_seq, hd), F32)),
-            in_specs=[smem, vmem, hbm, hbm, hbm, hbm, hbm, hbm],
-            out_specs=(vmem,) * 4,
+            in_specs=[smem] + [hbm] * 7,
+            out_specs=(hbm, vmem, hbm, hbm),
             scratch_shapes=[
+                pltpu.VMEM(tokens.shape, BF16), pltpu.VMEM((n_blocks, nh, width), BF16),
+                pltpu.VMEM((n_seq, hd), F32), pltpu.VMEM((n_seq, hd), F32),
                 pltpu.VMEM((2, n_seq * heads, 128), F32),
                 pltpu.VMEM((groups, 2, 2, rows_d, 128), F32),
                 pltpu.VMEM((groups, 2, rows_d, 128), F32),
@@ -375,7 +403,7 @@
                 dma((groups, 3)), dma((groups, 3)),
                 dma((groups, 3)), dma((groups, 3)),
                 dma((groups, 3)), dma((groups, 3)),
-                dma((groups,)), dma((groups,)),
+                dma((groups,)), dma((groups,)), dma((groups,)),
             ],
             compiler_params=pltpu.CompilerParams(collective_id=0, has_side_effects=True,
                                                  vmem_limit_bytes=VMEM_A),
@@ -385,12 +413,13 @@
         k_upd, v_upd, y, _ = pl.pallas_call(
             functools.partial(write_kernel, (n_seq, seq_local, n_blocks, slots)),
             out_shape=(jax.ShapeDtypeStruct(k_cache.shape, BF16),) * 2 + (jax.ShapeDtypeStruct(y.shape, BF16), held),
-            in_specs=[smem, vmem, vmem, vmem, vmem, hbm, hbm],
+            in_specs=[smem, hbm, hbm, hbm, vmem, hbm, hbm],
             out_specs=(hbm, hbm, hbm, vmem),
             input_output_aliases={4: 3},
             scratch_shapes=[
+                pltpu.VMEM((n_seq, hd), F32), pltpu.VMEM((n_seq, hd), F32), pltpu.VMEM(y.shape, BF16),
                 pltpu.VMEM((RING, nh // 2, seq_local, hd), BF16), pltpu.VMEM((RING, nh // 2, seq_local, hd), BF16),
-                dma((2, RING)), dma((2, RING)), dma((2, slots)), dma,
+                dma((2, RING)), dma((2, RING)), dma((2, slots)), dma((3,)),
             ],
             compiler_params=pltpu.CompilerParams(vmem_limit_bytes=VMEM_B),
         )(positions, k_new, v_new, y, kept, k_cache, v_cache)

time: 79.2 us -> 75.9 us (0.958)
  Pallas kernels: 78.3 us -> 74.9 us
    pallas_call x1, Pallas kernels: 49.8 us -> 47.2 us  [local_step(): pl.pallas_call(functools.partial(attend_kernel, (heads, seq_local, hd, gr...]
    pallas_call x1, Pallas kernels: 28.6 us -> 27.7 us  [local_step(): pl.pallas_call(functools.partial(write_kernel, (n_seq, seq_local, n_block...]
where the time goes in v4:
time: 75.9 us; the launch traced here: 75.6 us
  Pallas kernels  74.9 us (99%)
    pallas_call x1, Pallas kernels, local_step(): pl.pallas_call(functools.partial(attend_kernel, (heads, seq_local, hd, gr...  47.2 us
    pallas_call x1, Pallas kernels, local_step(): pl.pallas_call(functools.partial(write_kernel, (n_seq, seq_local, n_block...  27.7 us

profile of v4, /device:TPU:0, one launch (start us, length us, event | category | flops | bytes accessed | tf_op | source)
XLA Modules:
  0.0 75.6 jit_solution(16988555065439673393)
XLA Ops:
  0.6 47.2 %shard_map.103 = (bf16[16,16,2048]{2,1,0:T(8,128)(2,1)}, bf16[2,12,16,256,256]{4,3,2,1,0:T(8,128)(2,1)S(1)}, f32[256,256]{1,0:T(8,128)}, f32[256,256]{1,0:T(8,128)}) custom-call(s32[256]{0:T(256)} %pos_ref.3, bf16[256,2048]{1,0:T(8,128)(2,1)} %x_hbm.1, bf16[8,256,2048]{2,1,0:T(8,128)(2,1)} %bitcast.4, bf16[8,256,256]{2,1,0:T(8,128)(2,1)} %bitcast.5, ...), custom_call_target="tpu_custom_call" | custom-call | tf_op jit(solution)/shard_map/pallas_call | solution.py:384
  47.9 27.7 %shard_map.104 = (bf16[256,256,256]{2,1,0:T(8,128)(2,1)}, bf16[256,256,256]{2,1,0:T(8,128)(2,1)}, bf16[16,16,2048]{2,1,0:T(8,128)(2,1)}, bf16[2,12,16,256,256]{4,3,2,1,0:T(8,128)(2,1)S(1)}) custom-call(s32[256]{0:T(256)} %pos_ref.3, f32[256,256]{1,0:T(8,128)} %get-tuple-element.10.kn_hbm, ...), custom_call_target="tpu_custom_call", output_to_operand_aliasing={{3}: (4, {})} | custom-call | tf_op jit(solution)/shard_map/pallas_call | solution.py:413

commit v5 on v4

--- a/solution.py
+++ b/solution.py
@@ -12,13 +12,14 @@
 FLOOR = -1e30
 HALF = 16
 RING = 4
+DIRECT = 1
 LAG_C, LAG_S, LAG_R, LAG_Y = 4, 7, 10, 12
 
 
 def attend_kernel(dims, pos_ref, x_hbm, wq_hbm, wk_hbm, wv_hbm, wo_hbm, k_hbm, v_hbm,
                   y_hbm, held, kn_hbm, vn_hbm,
-                  x_ref, y_ref, kn_ref, vn_ref, q_ref, part, got_d, mix, got_1, obuf, wcol, sem_k, sem_v, sem_w, snd_w, rcv_w, snd_v, rcv_v,
-                  snd_d, rcv_d, snd_1, rcv_1, snd_2, rcv_2, snd_3, rcv_3, snd_r, rcv_r, sem_y):
+                  y_ref, kn_ref, vn_ref, q_ref, part, got_d, mix, got_1, obuf, wcol, sem_k, sem_v, sem_w, snd_w, rcv_w, snd_v, rcv_v,
+                  snd_d, rcv_d, snd_1, rcv_1, snd_2, rcv_2, snd_3, rcv_3, snd_r, rcv_r, sem_y, sem_x):
     heads, seq_local, hd, groups, slots = dims
     nh = HALF
     width = wo_hbm.shape[1]
@@ -53,16 +54,19 @@
     def staged(w):
         return held.at[lax.rem(w, 4) // 2, first_stage + w // 4, pl.ds(lax.rem(w, 2) * 8, 8)]
 
-    x_copy = pltpu.make_async_copy(x_hbm, x_ref, sem_w.at[n_tiles + 1])
-    x_copy.start()
+    rows_x = x_hbm.shape[0]
+    x_cuts = [held.at[1, slots - 1, i] for i in range(8)]
+    x_copies = [pltpu.make_async_copy(x_hbm.at[:, pl.ds(i * hd, hd)], x_cuts[i], sem_x.at[i]) for i in range(8)]
+    for cp in x_copies:
+        cp.start()
     for w in range(n_tiles):
         src = wq_hbm.at[:, :, pl.ds(w * hd, hd)] if w < heads else (wk_hbm, wv_hbm)[w - heads]
         pltpu.make_async_copy(src, staged(w), sem_w.at[w]).start()
 
     gate = pltpu.get_barrier_semaphore()
-    for k in (1, 2, 4, 6):
+    for k in range(1, 8):
         pl.semaphore_signal(gate, inc=1, device_id=peer(k), device_id_type=MESH)
-    pl.semaphore_wait(gate, 4)
+    pl.semaphore_wait(gate, 7)
 
     own_w = pltpu.make_async_copy(wo_hbm.at[:, columns(chip)], wcol.at[me], sem_w.at[n_tiles])
 
@@ -79,27 +83,31 @@
     own_w.start()
 
     def d_copy(g):
-        return remote(part.at[g, 1 - core], got_d.at[g], snd_d.at[g], rcv_d.at[g], 1)
+        return remote(part.at[g, 1 - core], got_d.at[g], snd_d, rcv_d.at[g], 1)
 
     def one_copy(g, k):
         return remote(mix.at[g, jnp.bitwise_xor(chip, k)], got_1.at[g, k - 1],
-                      snd_1.at[g, k - 1], rcv_1.at[g, k - 1], 2 * k)
+                      snd_1, rcv_1.at[g], 2 * k)
 
     def two_copy(g, k):
         block = obuf.at[g, :, columns(chip)]
-        return remote(block, block, snd_2.at[g, k - 1], rcv_2.at[g, k - 1], 2 * k)
+        return remote(block, block, snd_2, rcv_2.at[g], 2 * k)
 
     def three_copy(g, k):
         block = y_ref.at[2 * g + core, :, columns(chip)]
-        return remote(block, block, snd_3.at[g, k - 1], rcv_3.at[g, k - 1], 2 * k)
+        return remote(block, block, snd_3, rcv_3.at[g], 2 * k)
+
+    def far_copy(g, k):
+        block = y_ref.at[2 * g + core, :, columns(chip)]
+        return remote(block, block, snd_r, rcv_r.at[g], 2 * k + 1)
 
     def relay_copy(g):
         rows = y_ref.at[2 * g + core]
-        return remote(rows, rows, snd_r.at[g], rcv_r.at[g], 1)
+        return remote(rows, rows, snd_r, rcv_r.at[g], 1)
 
     def y_copy(g):
         rows = pl.ds(2 * g, 2)
-        return pltpu.make_async_copy(y_ref.at[rows], y_hbm.at[rows], sem_y.at[g])
+        return pltpu.make_async_copy(y_ref.at[rows], y_hbm.at[rows], sem_y)
 
     def tile(w, c):
         pltpu.make_async_copy(wk_hbm, staged(w), sem_w.at[w]).wait()
@@ -107,13 +115,13 @@
         @pl.when(w < first_stage)
         def _():
             load(w)
-        wt = staged(w)[...].reshape(x_ref.shape[1], hd)
-        acc = jnp.dot(x_ref[...], wt, preferred_element_type=F32)
+        wt = staged(w)
+        acc = sum(jnp.dot(x_cuts[i][...], wt[i], preferred_element_type=F32) for i in range(8))
 
         @pl.when(w < heads)
         def _():
             for z in range(2):
-                q_ref[z, pl.ds(w, x_ref.shape[0], stride=heads), :] = acc[:, z * 128:(z + 1) * 128]
+                q_ref[z, pl.ds(w, rows_x, stride=heads), :] = acc[:, z * 128:(z + 1) * 128]
 
         @pl.when(w == heads)
         def _():
@@ -124,7 +132,8 @@
             vn_ref[...] = acc.astype(BF16).astype(F32)
         return c
 
-    x_copy.wait()
+    for cp in x_copies:
+        cp.wait()
     lax.fori_loop(0, n_tiles, tile, 0)
     kn_out = pltpu.make_async_copy(kn_ref, kn_hbm, sem_w.at[n_tiles])
     vn_out = pltpu.make_async_copy(vn_ref, vn_hbm, sem_w.at[n_tiles + 1])
@@ -193,8 +202,7 @@
             mix[g, c, 4 * nh:4 * nh + 8, :] = jnp.concatenate([m[mine], total[mine], m[:4]], axis=0)
 
     def combine(g):
-        for k in (1, 2, 3):
-            one_copy(g, k).wait_recv()
+        remote(got_1.at[g], got_1.at[g], snd_1, rcv_1.at[g], 2).wait_recv()
         parts = [mix.at[g, chip]] + [got_1.at[g, k] for k in range(3)]
         stats = [r[4 * nh:4 * nh + 8, :] for r in parts]
         m = functools.reduce(jnp.maximum, stats)
@@ -211,8 +219,8 @@
         obuf[g, :, columns(chip)] = jnp.concatenate(outs, axis=1).astype(BF16)
 
     def project(g):
-        for k in (1, 2, 3):
-            two_copy(g, k).wait_recv()
+        three = obuf.at[g, :, pl.ds(0, 3 * quarter)]
+        remote(three, three, snd_2, rcv_2.at[g], 2).wait_recv()
         y = jnp.dot(obuf[g], wcol[...].reshape(width, quarter), preferred_element_type=F32)
         y_ref[2 * g + core, :, columns(chip)] = y.astype(BF16)
 
@@ -255,11 +263,19 @@
             for k in (3, 1, 2):
                 three_copy(it - LAG_S, k).start()
 
+            @pl.when(it - LAG_S >= groups - DIRECT)
+            def _():
+                for k in (3, 1, 2, 0):
+                    far_copy(it - LAG_S, k).start()
+
         @pl.when(jnp.logical_and(it >= LAG_R, it < groups + LAG_R))
         def _():
-            for k in (1, 2, 3):
-                three_copy(it - LAG_R, k).wait_recv()
-            relay_copy(it - LAG_R).start()
+            three = y_ref.at[2 * (it - LAG_R) + core, :, pl.ds(0, 3 * quarter)]
+            remote(three, three, snd_3, rcv_3.at[it - LAG_R], 2).wait_recv()
+
+            @pl.when(it - LAG_R < groups - DIRECT)
+            def _():
+                relay_copy(it - LAG_R).start()
 
         @pl.when(it >= LAG_Y)
         def _():
@@ -271,17 +287,13 @@
     kn_out.wait()
     vn_out.wait()
 
-    def finish(g, carry):
-        relay_copy(g).wait_send()
-        y_copy(g).wait()
-        d_copy(g).wait_send()
-        for k in (1, 2, 3):
-            one_copy(g, k).wait_send()
-            two_copy(g, k).wait_send()
-            three_copy(g, k).wait_send()
-        return carry
-
-    lax.fori_loop(0, groups, finish, 0)
+    blocks = pl.ds(0, 3)
+    for sent, sem in ((part.at[:, 0], snd_d), (mix.at[:, blocks], snd_1),
+                      (obuf.at[:, :, pl.ds(0, 3 * quarter)], snd_2),
+                      (y_ref.at[pl.ds(0, groups), :, pl.ds(0, 3 * quarter)], snd_3),
+                      (y_ref.at[pl.ds(0, groups)], snd_r)):
+        remote(sent, sent, sem, rcv_d.at[0], 1).wait_send()
+    pltpu.make_async_copy(y_ref, y_hbm, sem_y).wait()
 
 
 def write_kernel(dims, pos_ref, kn_hbm, vn_hbm, y_in, _, k_hbm, v_hbm, ko_hbm, vo_hbm, y_hbm, held,
@@ -372,7 +384,7 @@
         nh = HALF
         groups = n_seq // (2 * nh)
         n_blocks = 2 * groups
-        slots = n_blocks * 3 // 4
+        slots = n_blocks * 13 // 16
         vmem, hbm = pl.BlockSpec(memory_space=pltpu.VMEM), pl.BlockSpec(memory_space=pl.ANY)
         smem = pl.BlockSpec(memory_space=pltpu.SMEM)
         dma = pltpu.SemaphoreType.DMA
@@ -388,7 +400,7 @@
             in_specs=[smem] + [hbm] * 7,
             out_specs=(hbm, vmem, hbm, hbm),
             scratch_shapes=[
-                pltpu.VMEM(tokens.shape, BF16), pltpu.VMEM((n_blocks, nh, width), BF16),
+                pltpu.VMEM((n_blocks, nh, width), BF16),
                 pltpu.VMEM((n_seq, hd), F32), pltpu.VMEM((n_seq, hd), F32),
                 pltpu.VMEM((2, n_seq * heads, 128), F32),
                 pltpu.VMEM((groups, 2, 2, rows_d, 128), F32),
@@ -399,11 +411,8 @@
                 pltpu.VMEM((heads, w_out.shape[0], width // 4), BF16),
                 dma((slots,)), dma((slots,)), dma((n_stage,)),
                 dma((3,)), dma((3,)), dma((4,)), dma((4,)),
-                dma((groups,)), dma((groups,)),
-                dma((groups, 3)), dma((groups, 3)),
-                dma((groups, 3)), dma((groups, 3)),
-                dma((groups, 3)), dma((groups, 3)),
-                dma((groups,)), dma((groups,)), dma((groups,)),
+                dma, dma((groups,)), dma, dma((groups,)), dma, dma((groups,)), dma, dma((groups,)),
+                dma, dma((groups,)), dma, dma((8,)),
             ],
             compiler_params=pltpu.CompilerParams(collective_id=0, has_side_effects=True,
                                                  vmem_limit_bytes=VMEM_A),
@@ -429,5 +438,5 @@
     return jax.shard_map(local_step, mesh=mesh, in_specs=(P('dp', None), P(), P(), P(), P('sp', None), cache_spec, cache_spec, P('dp')), out_specs=(P('dp', None), cache_spec, cache_spec), check_vma=False)
 
 
-VMEM_A = 14 << 20
-VMEM_B = 12 << 20
+VMEM_A = int(11.6 * 2**20)
+VMEM_B = 10 << 20

time: 75.9 us -> 73 us (0.962)
  Pallas kernels: 74.9 us -> 72.2 us
    pallas_call x1, Pallas kernels: 27.7 us -> 26.2 us  [local_step(): pl.pallas_call(functools.partial(write_kernel, (n_seq, seq_local, n_block...]
    pallas_call x1, Pallas kernels: 47.2 us -> 46 us  [local_step(): pl.pallas_call(functools.partial(attend_kernel, (heads, seq_local, hd, gr...]
where the time goes in v5:
time: 73 us; the launch traced here: 72.8 us
  Pallas kernels  72.2 us (99%)
    pallas_call x1, Pallas kernels, local_step(): pl.pallas_call(functools.partial(attend_kernel, (heads, seq_local, hd, gr...  46 us
    pallas_call x1, Pallas kernels, local_step(): pl.pallas_call(functools.partial(write_kernel, (n_seq, seq_local, n_block...  26.2 us

profile of v5, /device:TPU:0, one launch (start us, length us, event | category | flops | bytes accessed | tf_op | source)
XLA Modules:
  0.0 72.8 jit_solution(7890348917915210027)
XLA Ops:
  0.6 46.0 %shard_map.103 = (bf16[16,16,2048]{2,1,0:T(8,128)(2,1)}, bf16[2,13,16,256,256]{4,3,2,1,0:T(8,128)(2,1)S(1)}, f32[256,256]{1,0:T(8,128)}, f32[256,256]{1,0:T(8,128)}) custom-call(s32[256]{0:T(256)} %pos_ref.3, bf16[256,2048]{1,0:T(8,128)(2,1)} %x_hbm.1, bf16[8,256,2048]{2,1,0:T(8,128)(2,1)} %bitcast.4, bf16[8,256,256]{2,1,0:T(8,128)(2,1)} %bitcast.5, ...), custom_call_target="tpu_custom_call" | custom-call | tf_op jit(solution)/shard_map/pallas_call | solution.py:396
  46.6 26.2 %shard_map.104 = (bf16[256,256,256]{2,1,0:T(8,128)(2,1)}, bf16[256,256,256]{2,1,0:T(8,128)(2,1)}, bf16[16,16,2048]{2,1,0:T(8,128)(2,1)}, bf16[2,13,16,256,256]{4,3,2,1,0:T(8,128)(2,1)S(1)}) custom-call(s32[256]{0:T(256)} %pos_ref.3, f32[256,256]{1,0:T(8,128)} %get-tuple-element.10.kn_hbm, ...), custom_call_target="tpu_custom_call", output_to_operand_aliasing={{3}: (4, {})} | custom-call | tf_op jit(solution)/shard_map/pallas_call | solution.py:422

commit v6 on v5

--- a/solution.py
+++ b/solution.py
@@ -13,7 +13,7 @@
 HALF = 16
 RING = 4
 DIRECT = 1
-LAG_C, LAG_S, LAG_R, LAG_Y = 4, 7, 10, 12
+LAG_C, LAG_S, LAG_R, LAG_Y = 3, 6, 9, 10
 
 
 def attend_kernel(dims, pos_ref, x_hbm, wq_hbm, wk_hbm, wv_hbm, wo_hbm, k_hbm, v_hbm,

time: 73 us -> 73 us (level)
  no operation moved by 1% of the time
where the time goes in v6:
time: 73 us; the launch traced here: 72.8 us
  Pallas kernels  72.1 us (99%)
    pallas_call x1, Pallas kernels, local_step(): pl.pallas_call(functools.partial(attend_kernel, (heads, seq_local, hd, gr...  45.9 us
    pallas_call x1, Pallas kernels, local_step(): pl.pallas_call(functools.partial(write_kernel, (n_seq, seq_local, n_block...  26.2 us

profile of v6, /device:TPU:0, one launch (start us, length us, event | category | flops | bytes accessed | tf_op | source)
XLA Modules:
  0.0 72.8 jit_solution(5063626943610919482)
XLA Ops:
  0.6 45.9 %shard_map.103 = (bf16[16,16,2048]{2,1,0:T(8,128)(2,1)}, bf16[2,13,16,256,256]{4,3,2,1,0:T(8,128)(2,1)S(1)}, f32[256,256]{1,0:T(8,128)}, f32[256,256]{1,0:T(8,128)}) custom-call(s32[256]{0:T(256)} %pos_ref.3, bf16[256,2048]{1,0:T(8,128)(2,1)} %x_hbm.1, bf16[8,256,2048]{2,1,0:T(8,128)(2,1)} %bitcast.4, bf16[8,256,256]{2,1,0:T(8,128)(2,1)} %bitcast.5, ...), custom_call_target="tpu_custom_call" | custom-call | tf_op jit(solution)/shard_map/pallas_call | solution.py:396
  46.6 26.2 %shard_map.104 = (bf16[256,256,256]{2,1,0:T(8,128)(2,1)}, bf16[256,256,256]{2,1,0:T(8,128)(2,1)}, bf16[16,16,2048]{2,1,0:T(8,128)(2,1)}, bf16[2,13,16,256,256]{4,3,2,1,0:T(8,128)(2,1)S(1)}) custom-call(s32[256]{0:T(256)} %pos_ref.3, f32[256,256]{1,0:T(8,128)} %get-tuple-element.10.kn_hbm, ...), custom_call_target="tpu_custom_call", output_to_operand_aliasing={{3}: (4, {})} | custom-call | tf_op jit(solution)/shard_map/pallas_call | solution.py:422
